TPU v7x, 32 devices: a whole 2x2x4 slice. The times are simulated.
32 devices in a mesh: row: 4 (over x, core), col: 8 (over z, y).
Axes of the slice: x: 2, y: 2, z: 4, core: 2. Of those that a mesh axis runs over, the one named last changes fastest.
Arguments:
- resistance: float32 [4096, 8192], P('row', 'col'), may hold values from 1 to 100
- source_mask: int32 [4096, 8192], P('row', 'col'), may hold values 0 or 1
- target_mask: int32 [4096, 8192], P('row', 'col'), may hold values 0 or 1
- centers: int32 [512, 2], P(('row', 'col')), may hold values from 0 to 8191, as said below
- live_counts: int32 [32], P(('row', 'col')), may hold values from 1 to 16, 128 in all
Outputs:
- current_map: float32 [4096, 8192], P('row', 'col')
Inputs may be any that keep to these rules, and one draw needn't show every extreme that they name: `centers`: the center of slot s lies inside the block of raster cells held by device s // 16 (numbered along row+col, row slowest). Slots 0 to live_counts[d] - 1 of device d are live; some device has all 16 slots live.
All inputs are finite; a program needn't handle non-finite values. No bound on the sum of `source_mask` or of `target_mask` on one device may be relied on, other than what follows from the above.
Results may differ from a plain program's by a relative error of at most 0.0003.
Values sent between devices are 32-bit elements; how exact they have to be, the bound alone decides.
A program may use at most 128 MiB of HBM per device.

v0:
```python
import functools

import jax
import jax.numpy as jnp
from jax import lax
from jax.experimental import pallas as pl
from jax.experimental.pallas import tpu as pltpu
from jax.sharding import PartitionSpec as P

RAD = 64
SIDE = 2 * RAD
ITERS = 24
LEAKAGE = 0.02
GROUP = 4
LANES = 128
TALL = SIDE + 8
WIDE = 2 * LANES
SHIFTS = ((0, -1), (0, 1), (-1, 0), (1, 0), (-1, -1), (-1, 1), (1, -1), (1, 1))


def roll(value, shift, axis):
    return pltpu.roll(value, shift % value.shape[axis], axis)


def lane_ids(shape):
    return lax.broadcasted_iota(jnp.int32, shape, 1)


def to_low(packed):
    return packed, roll(packed, RAD, 1)


def to_high(packed):
    return roll(packed, RAD, 1), packed


def pack_low(tile):
    half = tile.shape[0] // 2
    first, second = tile[:half], tile[half:]
    return jnp.where(lane_ids(first.shape) < RAD, first, roll(second, RAD, 1))


def pack_high(tile):
    half = tile.shape[0] // 2
    first, second = tile[:half], tile[half:]
    return jnp.where(lane_ids(first.shape) < RAD, roll(first, RAD, 1), second)


def neighbours():
    row, col = lax.axis_index("row"), lax.axis_index("col")
    rows, cols = lax.axis_size("row"), lax.axis_size("col")
    found = {}
    for (dr, dc) in SHIFTS:
        r, c = row + dr, col + dc
        found[(dr, dc)] = ((r >= 0) & (r < rows) & (c >= 0) & (c < cols), (r, c))
    return found


def greet(found):
    barrier = pltpu.get_barrier_semaphore()
    for at in SHIFTS:
        exists, device = found[at]

        @pl.when(exists)
        def _():
            pl.semaphore_signal(barrier, inc=1, device_id=device, device_id_type=pl.DeviceIdType.MESH)


def all_greeted(found):
    count = sum(found[at][0].astype(jnp.int32) for at in SHIFTS)
    pl.semaphore_wait(pltpu.get_barrier_semaphore(), count)


def transfers(found, pieces, halos, send_sems, recv_sems):
    made = []
    for k, at in enumerate(SHIFTS):
        exists, device = found[at]
        back = (-at[0], -at[1])
        made.append((exists, pltpu.make_async_remote_copy(
            src_ref=pieces[at],
            dst_ref=halos[back],
            send_sem=send_sems.at[k],
            recv_sem=recv_sems.at[SHIFTS.index(back)],
            device_id=device,
            device_id_type=pl.DeviceIdType.MESH,
        )))
    return made


def landings(found, pieces, halos, send_sems, recv_sems):
    made = []
    for k, at in enumerate(SHIFTS):
        exists, device = found[at]
        made.append((exists, pltpu.make_async_remote_copy(
            src_ref=pieces[at],
            dst_ref=halos[at],
            send_sem=send_sems.at[k],
            recv_sem=recv_sems.at[k],
            device_id=device,
            device_id_type=pl.DeviceIdType.MESH,
        )))
    return made


def start_all(copies):
    for exists, copy in copies:
        pl.when(exists)(copy.start)


def finish_all(copies, arrivals):
    for exists, copy in copies:
        pl.when(exists)(copy.wait_send)
    for exists, copy in arrivals:
        pl.when(exists)(copy.wait_recv)


def corner_of(centers, slot, rows, cols):
    return lax.rem(centers[slot, 0], rows) - RAD, lax.rem(centers[slot, 1], cols) - RAD


def is_inner(top, left, rows, cols):
    return (top >= 0) & (top <= rows - SIDE) & (left >= 0) & (left <= cols - SIDE)


def clamped(top, left, rows, cols):
    row = jnp.clip((top + RAD) // 8 * 8 - RAD, 0, rows - TALL)
    col = jnp.clip((left + LANES) // LANES * LANES - LANES, 0, cols - WIDE)
    return pl.multiple_of(row, 8), pl.multiple_of(col, LANES)


def total(values):
    return jnp.sum(jnp.sum(values, axis=0, keepdims=True), axis=1, keepdims=True)


def cut_rows(value, skip):
    return pltpu.roll(value, lax.rem(TALL - skip, TALL), 0)[:SIDE]


def add_window(acc, current, top, left):
    col = pl.multiple_of((left + LANES) // LANES * LANES, LANES)
    shift = left + LANES - col
    wide = jnp.concatenate([current, jnp.zeros_like(current)], axis=1)
    wide = pltpu.roll(wide, shift, 1)
    wide = jnp.concatenate([wide, jnp.zeros((8, WIDE), jnp.float32)], axis=0)
    wide = pltpu.roll(wide, lax.rem(top + RAD, 8), 0)
    rows = pl.ds(pl.multiple_of((top + RAD) // 8 * 8, 8), TALL)
    acc[rows, pl.ds(col, WIDE)] = acc[rows, pl.ds(col, WIDE)] + wide


def solver_parts(state):
    r_s, p_s, s_s, x_s, w_s, vd_s, vu_s, hr_s, hl_s, isd_s, inj_s, gnd_s, v_s, h_s = state
    row_id = lax.broadcasted_iota(jnp.int32, (SIDE, SIDE), 0)
    col_id = lax.broadcasted_iota(jnp.int32, (SIDE, SIDE), 1)

    def operate(b):
        here = r_s[b, 8:8 + SIDE, :]
        down = r_s[b, 9:9 + SIDE, :]
        up = r_s[b, 7:7 + SIDE, :]
        beside = vd_s[b] * down + vu_s[b] * up
        beside = beside + hr_s[b] * roll(here, -1, 1) + hl_s[b] * roll(here, 1, 1)
        applied = here - beside
        w_s[b] = applied
        return total(here * here), total(here * applied)

    def prepare(b, res, signed):
        res_down, res_right = roll(res, -1, 0), roll(res, -1, 1)
        has_down = (res > 0.0) & (res_down > 0.0) & (row_id < SIDE - 1)
        has_right = (res > 0.0) & (res_right > 0.0) & (col_id < SIDE - 1)
        vertical = jnp.where(has_down, 2.0 / jnp.where(has_down, res + res_down, 1.0), 0.0)
        horizontal = jnp.where(has_right, 2.0 / jnp.where(has_right, res + res_right, 1.0), 0.0)
        center = ((row_id == RAD) & (col_id == RAD)).astype(jnp.float32)
        inject = jnp.maximum(signed, 0.0) + center
        ground = jnp.maximum(-signed, 0.0)
        diagonal = vertical + roll(vertical, 1, 0) + horizontal + roll(horizontal, 1, 1) + ground + LEAKAGE
        isd = 1.0 / jnp.sqrt(diagonal)
        scaled_v = vertical * isd * roll(isd, -1, 0)
        scaled_h = horizontal * isd * roll(isd, -1, 1)
        v_s[b], h_s[b] = vertical, horizontal
        vd_s[b], vu_s[b] = scaled_v, roll(scaled_v, 1, 0)
        hr_s[b], hl_s[b] = scaled_h, roll(scaled_h, 1, 1)
        inj_s[b], gnd_s[b], isd_s[b] = inject, ground, isd
        r_s[b, 0:8, :] = jnp.zeros((8, SIDE), jnp.float32)
        r_s[b, 8 + SIDE:16 + SIDE, :] = jnp.zeros((8, SIDE), jnp.float32)
        r_s[b, 8:8 + SIDE, :] = inject * isd
        zero = jnp.zeros((SIDE, SIDE), jnp.float32)
        p_s[b], s_s[b], x_s[b] = zero, zero, zero

    def step(_, carry):
        after = []
        for b in range(GROUP):
            alpha, beta, _, _ = carry[b]
            here = r_s[b, 8:8 + SIDE, :]
            direction = here + beta * p_s[b]
            applied = w_s[b] + beta * s_s[b]
            p_s[b] = direction
            s_s[b] = applied
            x_s[b] = x_s[b] + alpha * direction
            r_s[b, 8:8 + SIDE, :] = here - alpha * applied
        for b in range(GROUP):
            _, _, gamma_inv, alpha_inv = carry[b]
            gamma, delta = operate(b)
            beta = gamma * gamma_inv
            bottom = delta - beta * (gamma * alpha_inv)
            gamma_inv = 1.0 / gamma
            after.append((gamma / bottom, beta, gamma_inv, bottom * gamma_inv))
        return tuple(after)

    def finish(b):
        isd, vertical, horizontal = isd_s[b], v_s[b], h_s[b]
        voltage = x_s[b] * isd
        flow_down = vertical * jnp.abs(voltage - roll(voltage, -1, 0))
        flow_right = horizontal * jnp.abs(voltage - roll(voltage, -1, 1))
        flow = flow_down + roll(flow_down, 1, 0) + flow_right + roll(flow_right, 1, 1)
        return 0.5 * (flow + inj_s[b] + gnd_s[b] * jnp.abs(voltage))

    def iterate():
        carry = []
        for b in range(GROUP):
            gamma, delta = operate(b)
            gamma_inv = 1.0 / gamma
            carry.append((gamma / delta, jnp.zeros_like(gamma), gamma_inv, delta * gamma_inv))
        lax.fori_loop(0, ITERS, step, tuple(carry))

    return prepare, iterate, finish


def spans_of(rows, cols):
    return {
        -1: (slice(0, RAD), slice(0, LANES)),
        0: (slice(RAD, RAD + rows), slice(LANES, LANES + cols)),
        1: (slice(RAD + rows, SIDE + rows), slice(LANES + cols, WIDE + cols)),
    }


def turn_own(res, source, target, skip, turn):
    source, target = source.astype(jnp.float32), target.astype(jnp.float32)
    mark = source - target * (1.0 - source)
    turn = lax.rem(WIDE + turn, WIDE)
    res = cut_rows(pltpu.roll(res, turn, 1)[:, :SIDE], skip)
    mark = cut_rows(pltpu.roll(mark, turn, 1)[:, :SIDE], skip)
    return res, mark


def cut_kernel(rows, cols, centers, live, *refs):
    raw, out, bufs, sems = refs[:3], refs[3], refs[4:7], refs[7]

    def place(slot):
        top, left = corner_of(centers, slot, rows, cols)
        return top, left, *clamped(top, left, rows, cols)

    def copies(slot):
        _, _, row, col = place(slot)
        return [
            pltpu.make_async_copy(src.at[pl.ds(row, TALL), pl.ds(col, WIDE)], dst.at[slot], sems.at[k, slot])
            for k, (src, dst) in enumerate(zip(raw, bufs))
        ]

    def begin(slot, _):
        for copy in copies(slot):
            copy.start()
        return 0

    def cut(slot, _):
        for copy in copies(slot):
            copy.wait()
        top, left, row, col = place(slot)
        res, mark = turn_own(*(buf[slot] for buf in bufs), top - row, col - left)
        out[0, slot] = res
        out[1, slot] = mark / res
        return 0

    lax.fori_loop(0, live[0], begin, 0)
    lax.fori_loop(0, live[0], cut, 0)


def inner_kernel(rows, cols, windows, *refs):
    raw = refs[:3]
    cur, outs = refs[3], dict(zip(SHIFTS, refs[4:12]))
    pieces, halos = dict(zip(SHIFTS, refs[12:20])), dict(zip(SHIFTS, refs[20:28]))
    frames = [refs[28 + 3 * k:31 + 3 * k] for k in range(4)]
    sems, send_sems, recv_sems = refs[40:43]
    prepare, iterate, finish = solver_parts(refs[43:])
    slots = windows.shape[1]
    found = neighbours()

    everything = pl.ds(0, rows)
    places = (
        (everything, pl.ds(0, LANES)),
        (everything, pl.ds(cols - LANES, LANES)),
        (pl.ds(0, RAD), pl.ds(0, cols)),
        (pl.ds(rows - RAD, RAD), pl.ds(0, cols)),
    )
    frame_copies = [
        [pltpu.make_async_copy(raw[k].at[places[f]], frames[f][k], sems.at[f, k]) for k in range(3)]
        for f in range(4)
    ]
    for copy in sum(frame_copies, []):
        copy.start()
    for at in SHIFTS:
        halos[at][...] = jnp.zeros_like(halos[at])
    greet(found)

    def strengths(frame, cut=slice(None)):
        res, source, target = (ref[cut] for ref in frame)
        source, target = source.astype(jnp.float32), target.astype(jnp.float32)
        conduct = 1.0 / res
        return res, source * conduct - target * (1.0 - source) * conduct

    for f, at in enumerate(((0, -1), (0, 1), (-1, 0), (1, 0))):
        for copy in frame_copies[f]:
            copy.wait()
        for k, value in enumerate(strengths(frames[f])):
            if at[1] == 0:
                pieces[at][k] = value
            else:
                squeeze = pack_low if at[1] < 0 else pack_high
                pieces[at][k] = squeeze(value)
                pieces[(-1, at[1])][k] = squeeze(value[:RAD])
                pieces[(1, at[1])][k] = squeeze(value[rows - RAD:])
    all_greeted(found)
    copies = transfers(found, pieces, halos, send_sems, recv_sems)
    start_all(copies)

    def solve_group(group, _):
        def ready(b, _):
            slot = group * GROUP + b
            prepare(b, windows[0, slot], windows[1, slot])
            return 0

        lax.fori_loop(0, GROUP, ready, 0)
        iterate()

        def done(b, _):
            cur[group * GROUP + b] = finish(b)
            return 0

        lax.fori_loop(0, GROUP, done, 0)
        return 0

    lax.fori_loop(0, slots // GROUP, solve_group, 0)
    finish_all(copies, landings(found, pieces, halos, send_sems, recv_sems))
    for at in SHIFTS:
        outs[at][...] = halos[at][...]


def return_kernel(*refs):
    pieces, outs, halos = (dict(zip(SHIFTS, refs[8 * k:8 * k + 8])) for k in range(3))
    send_sems, recv_sems = refs[24:]
    found = neighbours()
    for at in SHIFTS:
        halos[at][...] = jnp.zeros_like(halos[at])
    greet(found)
    all_greeted(found)
    copies = transfers(found, pieces, halos, send_sems, recv_sems)
    start_all(copies)
    finish_all(copies, landings(found, pieces, halos, send_sems, recv_sems))
    for at in SHIFTS:
        outs[at][...] = halos[at][...]


def border_kernel(rows, cols, centers, live, inner_cur, *refs):
    raw, halos = refs[:3], dict(zip(SHIFTS, refs[3:11]))
    out, outs = refs[11], dict(zip(SHIFTS, refs[12:20]))
    bufs, sems, order, ext, acc, out_sem = refs[20:23], *refs[23:28]
    prepare, iterate, finish = solver_parts(refs[28:])

    def copies(slot):
        top, left = corner_of(centers, slot, rows, cols)
        row, col = clamped(top, left, rows, cols)
        return [
            pltpu.make_async_copy(
                src.at[pl.ds(row, TALL), pl.ds(col, WIDE)],
                dst.at[slot, pl.ds(RAD, TALL), :],
                sems.at[k, slot],
            )
            for k, (src, dst) in enumerate(zip(raw, bufs))
        ]

    def classify(slot, count):
        top, left = corner_of(centers, slot, rows, cols)
        outer = jnp.logical_not(is_inner(top, left, rows, cols))

        @pl.when(outer)
        def _():
            order[count] = slot
            for copy in copies(slot):
                copy.start()

        return count + outer.astype(jnp.int32)

    count = lax.fori_loop(0, live[0], classify, jnp.int32(0))
    acc[...] = jnp.zeros_like(acc)
    spans = spans_of(rows, cols)
    for which in range(2):
        for dr in (-1, 1):
            ext[which, spans[dr][0], spans[0][1]] = halos[(dr, 0)][which]
        for dr in (-1, 0, 1):
            start, stop = spans[dr][0].start, spans[dr][0].stop
            middle = (start + stop) // 2
            for dc in (-1, 1):
                split = to_high if dc < 0 else to_low
                first, second = split(halos[(dr, dc)][which])
                ext[which, start:middle, spans[dc][1]] = first
                ext[which, middle:stop, spans[dc][1]] = second

    row_id = lax.broadcasted_iota(jnp.int32, (SIDE, SIDE), 0)
    col_id = lax.broadcasted_iota(jnp.int32, (SIDE, SIDE), 1)

    def fetch(slot):
        top, left = corner_of(centers, slot, rows, cols)
        row, col = clamped(top, left, rows, cols)
        take = pl.ds(pl.multiple_of((RAD + top - row) // 8 * 8, 8), TALL)
        res, source, target = (buf[slot, take, :] for buf in bufs)
        res, mark = turn_own(res, source, target, lax.rem(RAD + top - row, 8), col - left)
        at_row, at_col = row_id + top, col_id + left
        own = (at_row >= 0) & (at_row < rows) & (at_col >= 0) & (at_col < cols)
        base = pl.multiple_of((left + LANES) // LANES * LANES, LANES)
        back = lax.rem(WIDE + base - left - LANES, WIDE)
        span = pl.ds(pl.multiple_of((top + RAD) // 8 * 8, 8), TALL)
        outer = [
            cut_rows(pltpu.roll(ext[k, span, pl.ds(base, WIDE)], back, 1)[:, :SIDE], lax.rem(top + RAD, 8))
            for k in range(2)
        ]
        signed = jnp.where(own, mark / jnp.where(own, res, 1.0), outer[1])
        return jnp.where(own, res, outer[0]), signed

    def solve_group(group, _):
        def ready(b, _):
            at = group * GROUP + b
            slot = order[jnp.minimum(at, count - 1)]

            @pl.when(at < count)
            def _():
                for copy in copies(slot):
                    copy.wait()

            prepare(b, *fetch(slot))
            return 0

        lax.fori_loop(0, GROUP, ready, 0)
        iterate()

        def done(b, _):
            at = group * GROUP + b

            @pl.when(at < count)
            def _():
                top, left = corner_of(centers, order[at], rows, cols)
                add_window(acc, finish(b), top, left)

            return 0

        lax.fori_loop(0, GROUP, done, 0)
        return 0

    lax.fori_loop(0, (count + GROUP - 1) // GROUP, solve_group, 0)

    def place(slot, _):
        top, left = corner_of(centers, slot, rows, cols)

        @pl.when(is_inner(top, left, rows, cols))
        def _():
            add_window(acc, inner_cur[slot], top, left)

        return 0

    lax.fori_loop(0, live[0], place, 0)
    copy = pltpu.make_async_copy(acc.at[pl.ds(RAD, rows), pl.ds(LANES, cols)], out, out_sem)
    copy.start()
    for dr in (-1, 1):
        outs[(dr, 0)][...] = acc[spans[dr][0], spans[0][1]]
    for dr in (-1, 0, 1):
        for dc in (-1, 1):
            tile = acc[spans[dr][0], spans[dc][1]]
            outs[(dr, dc)][...] = pack_high(tile) if dc < 0 else pack_low(tile)
    copy.wait()


def fold_kernel(rows, cols, *refs):
    halos = dict(zip(SHIFTS, refs[1:9]))
    out, upper, lower, left, right, sems = refs[9:]
    last = cols - LANES
    inner_rows = rows - SIDE
    places = (
        (upper, pl.ds(0, RAD), pl.ds(0, cols)),
        (lower, pl.ds(rows - RAD, RAD), pl.ds(0, cols)),
        (left, pl.ds(RAD, inner_rows), pl.ds(0, LANES)),
        (right, pl.ds(RAD, inner_rows), pl.ds(last, LANES)),
    )
    fetch = [pltpu.make_async_copy(out.at[r, c], buf, sems.at[0, k]) for k, (buf, r, c) in enumerate(places)]
    store = [pltpu.make_async_copy(buf, out.at[r, c], sems.at[1, k]) for k, (buf, r, c) in enumerate(places)]
    for copy in fetch:
        copy.start()

    def spread(dr, dc):
        first, second = (to_low if dc < 0 else to_high)(halos[(dr, dc)][...])
        low = lane_ids(first.shape) < RAD
        keep = low if dc < 0 else jnp.logical_not(low)
        return jnp.where(keep, first, 0.0), jnp.where(keep, second, 0.0)

    for copy in fetch:
        copy.wait()
    half = rows // 2
    for dc, buf, at in ((-1, left, 0), (1, right, last)):
        first, second = spread(0, dc)
        buf[0:half - RAD] = buf[0:half - RAD] + first[RAD:]
        buf[half - RAD:inner_rows] = buf[half - RAD:inner_rows] + second[:half - RAD]
        upper[:, at:at + LANES] = upper[:, at:at + LANES] + first[:RAD]
        lower[:, at:at + LANES] = lower[:, at:at + LANES] + second[half - RAD:]
        for dr, strip in ((-1, upper), (1, lower)):
            one, two = spread(dr, dc)
            strip[:RAD // 2, at:at + LANES] = strip[:RAD // 2, at:at + LANES] + one
            strip[RAD // 2:, at:at + LANES] = strip[RAD // 2:, at:at + LANES] + two
    upper[...] = upper[...] + halos[(-1, 0)][...]
    lower[...] = lower[...] + halos[(1, 0)][...]
    for copy in store:
        copy.start()
    for copy in store:
        copy.wait()


def local(resistance, source_mask, target_mask, centers, live_counts):
    rows, cols = resistance.shape
    slots = centers.shape[0]
    f32, i32 = jnp.float32, jnp.int32
    smem = pl.BlockSpec(memory_space=pltpu.SMEM)
    vmem = pl.BlockSpec(memory_space=pltpu.VMEM)
    hbm = pl.BlockSpec(memory_space=pltpu.HBM)

    shapes = {
        at: (RAD if at[0] else rows, cols) if at[1] == 0 else ((RAD if at[0] else rows) // 2, LANES) for at in SHIFTS
    }
    pairs = [pltpu.VMEM((2, *shapes[at]), f32) for at in SHIFTS]
    strips = [pltpu.VMEM(shapes[at], f32) for at in SHIFTS]
    state = [pltpu.VMEM((GROUP, SIDE + 16, SIDE), f32)] + [pltpu.VMEM((GROUP, SIDE, SIDE), f32)] * 13
    kinds = (f32, i32, i32)
    frame_shapes = ((rows, LANES), (rows, LANES), (RAD, cols), (RAD, cols))

    windows = pl.pallas_call(
        functools.partial(cut_kernel, rows, cols),
        out_shape=jax.ShapeDtypeStruct((2, slots, SIDE, SIDE), f32),
        in_specs=[smem, smem, hbm, hbm, hbm],
        out_specs=vmem,
        scratch_shapes=[pltpu.VMEM((slots, TALL, WIDE), kind) for kind in kinds]
        + [pltpu.SemaphoreType.DMA((3, slots))],
        compiler_params=pltpu.CompilerParams(vmem_limit_bytes=57 << 20),
        name="cut",
    )(centers, live_counts, resistance, source_mask, target_mask)

    inner_cur, *halos = pl.pallas_call(
        functools.partial(inner_kernel, rows, cols),
        out_shape=[jax.ShapeDtypeStruct((slots, SIDE, SIDE), f32)]
        + [jax.ShapeDtypeStruct((2, *shapes[at]), f32) for at in SHIFTS],
        in_specs=[vmem, hbm, hbm, hbm],
        out_specs=[vmem] * 9,
        scratch_shapes=pairs
        + pairs
        + [pltpu.VMEM(shape, kind) for shape in frame_shapes for kind in kinds]
        + [pltpu.SemaphoreType.DMA((4, 3)), pltpu.SemaphoreType.DMA((8,)), pltpu.SemaphoreType.DMA((8,))]
        + state,
        compiler_params=pltpu.CompilerParams(vmem_limit_bytes=51 << 20, collective_id=0, has_side_effects=True),
        name="inner",
    )(windows, resistance, source_mask, target_mask)

    merged, *currents = pl.pallas_call(
        functools.partial(border_kernel, rows, cols),
        out_shape=[jax.ShapeDtypeStruct((rows, cols), f32)]
        + [jax.ShapeDtypeStruct(shapes[at], f32) for at in SHIFTS],
        in_specs=[smem, smem, vmem, hbm, hbm, hbm] + [vmem] * 8,
        out_specs=[hbm] + [vmem] * 8,
        scratch_shapes=[pltpu.VMEM((slots, TALL + SIDE, WIDE), kind) for kind in kinds]
        + [
            pltpu.SemaphoreType.DMA((3, slots)),
            pltpu.SMEM((slots,), i32),
            pltpu.VMEM((2, rows + SIDE, cols + WIDE), f32),
            pltpu.VMEM((rows + SIDE, cols + WIDE), f32),
            pltpu.SemaphoreType.DMA,
        ]
        + state,
        compiler_params=pltpu.CompilerParams(vmem_limit_bytes=45 << 20),
        name="border",
    )(centers, live_counts, inner_cur, resistance, source_mask, target_mask, *halos)

    back = pl.pallas_call(
        return_kernel,
        out_shape=[jax.ShapeDtypeStruct(shapes[at], f32) for at in SHIFTS],
        in_specs=[vmem] * 8,
        out_specs=[vmem] * 8,
        scratch_shapes=strips + [pltpu.SemaphoreType.DMA((8,)), pltpu.SemaphoreType.DMA((8,))],
        compiler_params=pltpu.CompilerParams(vmem_limit_bytes=8 << 20, collective_id=1, has_side_effects=True),
        name="give_back",
    )(*currents)
    out_shape = jax.ShapeDtypeStruct((rows, cols), f32)

    return pl.pallas_call(
        functools.partial(fold_kernel, rows, cols),
        out_shape=out_shape,
        in_specs=[hbm] + [vmem] * 8,
        out_specs=hbm,
        scratch_shapes=[
            pltpu.VMEM((RAD, cols), f32),
            pltpu.VMEM((RAD, cols), f32),
            pltpu.VMEM((rows - SIDE, LANES), f32),
            pltpu.VMEM((rows - SIDE, LANES), f32),
            pltpu.SemaphoreType.DMA((2, 4)),
        ],
        input_output_aliases={0: 0},
        compiler_params=pltpu.CompilerParams(vmem_limit_bytes=16 << 20),
        name="fold",
    )(merged, *back)


def solution(mesh):
    return jax.shard_map(
        local,
        mesh=mesh,
        in_specs=(
            P("row", "col"),
            P("row", "col"),
            P("row", "col"),
            P(("row", "col"), None),
            P(("row", "col")),
        ),
        out_specs=P("row", "col"),
        check_vma=False,
    )
```

profile of v0, /device:TPU:0, one launch (start us, length us, event | category | flops | bytes accessed | tf_op | source)
XLA Modules:
  0.0 99.2 jit_solution(686479924256109908)
XLA Ops:
  0.7 1.3 %copy.8.centers = s32[16,2]{1,0:T(8,128)} copy(s32[16,2]{0,1:T(2,128)} %param.8) | data formatting | bytes 256 | tf_op args[3]
  2.0 6.4 %cut.1.windows = f32[2,16,128,128]{3,2,1,0:T(8,128)} custom-call(s32[16,2]{1,0:T(8,128)} %copy.8.centers, s32[1]{0:T(128)S(6)} %copy.10.live, f32[1024,1024]{1,0:T(8,128)} %refs_0_.5, s32[1024,1024]{1,0:T(8,128)} %refs_1_.5, s32[1024,1024]{1,0:T(8,128)} %refs_2_.5), custom_call_target="tpu_custom_call" | custom-call | tf_op jit(solution)/shard_map/cut/pallas_call | solution.py:539
  8.4 0.0 copy-start
  8.4 0.0 copy-start.2
  8.4 48.1 %inner.1 = (f32[16,128,128]{2,1,0:T(8,128)}, f32[2,512,128]{2,1,0:T(8,128)S(1)}, f32[2,512,128]{2,1,0:T(8,128)S(1)}, f32[2,64,1024]{2,1,0:T(8,128)S(1)}, f32[2,6...) custom-call(f32[2,16,128,128]{3,2,1,0:T(8,128)} %cut.1.windows, ...), custom_call_target="tpu_custom_call" | custom-call | tf_op jit(solution)/shard_map/inner/pallas_call | solution.py:550
  56.5 0.0 copy-done
  56.6 0.0 copy-done.2
  56.6 0.0 copy-start.1
  56.6 1.2 %copy-done.1 = f32[16,128,128]{2,1,0:T(8,128)S(1)} copy-done((f32[16,128,128]{2,1,0:T(8,128)S(1)}, f32[16,128,128]{2,1,0:T(8,128)}, u32[]{:S(2)}) %copy-start.1) | copy-done | bytes 1048600
  57.8 29.6 %border.1 = (f32[1024,1024]{1,0:T(8,128)}, f32[512,128]{1,0:T(8,128)S(1)}, f32[512,128]{1,0:T(8,128)S(1)}, f32[64,1024]{1,0:T(8,128)S(1)}, f32[64,1024]{1,0:T(8,...) custom-call(s32[16,2]{1,0:T(8,128)S(1)} %copy-done.2, ...), custom_call_target="tpu_custom_call" | custom-call | tf_op jit(solution)/shard_map/border/pallas_call | solution.py:565
  87.4 9.1 %give_back.1 = (f32[512,128]{1,0:T(8,128)S(1)}, f32[512,128]{1,0:T(8,128)S(1)}, f32[64,1024]{1,0:T(8,128)S(1)}, f32[64,1024]{1,0:T(8,128)S(1)}, f32[32,128]{1,0:...) custom-call(f32[512,128]{1,0:T(8,128)S(1)} %get-tuple-element.41.refs_0_, ...), custom_call_target="tpu_custom_call" | custom-call | tf_op jit(solution)/shard_map/give_back/pallas_call | solution.py:584
  96.5 2.7 %fold.1 = f32[1024,1024]{1,0:T(8,128)} custom-call(f32[1024,1024]{1,0:T(8,128)} %get-tuple-element.40.refs_0_, f32[512,128]{1,0:T(8,128)S(1)} %get-tuple-element.49.refs_1_, f32[512,128]{1,0:T(8,128)S(1)} %get-tuple-element.50.refs_2_, f32[64,1024]{1,0:T(8,128)S(1)} %get-tuple-element.51.refs_3_, ...), custom_call_target="tpu_custom_call", output_to_operand_aliasing={{}: (0, {})} | custom-call | tf_op jit(solution)/shard_map/fold/pallas_call | solution.py:595
Async XLA Ops:
  8.4 48.1 %copy-start = (f32[1024,1024]{1,0:T(8,128)S(1)}, f32[1024,1024]{1,0:T(8,128)}, u32[]{:S(2)}) copy-start(f32[1024,1024]{1,0:T(8,128)} %refs_0_.5) | copy-start | bytes 12582916
  8.4 48.1 %copy-start.2 = (s32[16,2]{1,0:T(8,128)S(1)}, s32[16,2]{1,0:T(8,128)}, u32[]{:S(2)}) copy-start(s32[16,2]{1,0:T(8,128)} %copy.8.centers) | copy-start | bytes 388
  56.6 1.2 %copy-start.1 = (f32[16,128,128]{2,1,0:T(8,128)S(1)}, f32[16,128,128]{2,1,0:T(8,128)}, u32[]{:S(2)}) copy-start(f32[16,128,128]{2,1,0:T(8,128)} %get-tuple-element.31.inner_cur) | copy-start | bytes 3145732
where the time goes:
time: 99.6 us; the launch traced here: 99.2 us
  Pallas kernels  95.9 us (96%)
  local copies, waits for them, and re-layouts  2.57 us (3%)
    pallas_call x1, Pallas kernels, local(): pl.pallas_call(functools.partial(inner_kernel, rows, cols), out_shape=[ja...  48.1 us
    pallas_call x1, Pallas kernels, local(): pl.pallas_call(functools.partial(border_kernel, rows, cols), out_shape=[j...  29.6 us
    pallas_call x1, Pallas kernels, local(): pl.pallas_call(return_kernel, out_shape=[jax.ShapeDtypeStruct(shapes[at],...  9.12 us
    pallas_call x1, Pallas kernels, local(): pl.pallas_call(functools.partial(cut_kernel, rows, cols), out_shape=jax.S...  6.39 us
    pallas_call x1, Pallas kernels, local(): pl.pallas_call(functools.partial(fold_kernel, rows, cols), out_shape=out_...  2.68 us
    unnamed x7, local copies, waits for them, and re-layouts  2.57 us

commit v1 on v0

--- a/solution.py
+++ b/solution.py
@@ -11,7 +11,9 @@
 SIDE = 2 * RAD
 ITERS = 24
 LEAKAGE = 0.02
-GROUP = 4
+FAR = 1e37
+QUADS = 2
+GROUP = 4 * QUADS
 LANES = 128
 TALL = SIDE + 8
 WIDE = 2 * LANES
@@ -147,81 +149,284 @@
     acc[rows, pl.ds(col, WIDE)] = acc[rows, pl.ds(col, WIDE)] + wide
 
 
+PLANES = 4
+CHUNK = 64
+SEGMENTS = SIDE // PLANES
+EIGHTS = tuple(slice(8 * k, 8 * k + 8) for k in range(SIDE // 8))
+
+
+def lanes_of(shape):
+    return lax.broadcasted_iota(jnp.int32, shape, 1)
+
+
+def interleave(shape, transposed):
+    row, col = (lax.broadcasted_iota(jnp.int32, shape, axis) for axis in (0, 1))
+    if transposed:
+        row, col = col, row
+    window, place = row // SIDE, row % SIDE
+    return (col == (place % PLANES) * SIDE + window * SEGMENTS + place // PLANES).astype(jnp.bfloat16)
+
+
+def halves(value):
+    high = value.astype(jnp.bfloat16)
+    return high, (value - high.astype(jnp.float32)).astype(jnp.bfloat16)
+
+
+def mixed(parts, table):
+    found = jnp.dot(jnp.concatenate(parts, axis=0), table[...], preferred_element_type=jnp.float32)
+    size = parts[0].shape[0]
+    return [found[size * n:size * n + size] for n in range(len(parts))]
+
+
+def quad_state():
+    f32 = jnp.float32
+    planes = pltpu.VMEM((PLANES, SIDE, SIDE), f32)
+    padded = pltpu.VMEM((PLANES, SIDE + 16, SIDE), f32)
+    tile = pltpu.VMEM((SIDE, SIDE), f32)
+    table = pltpu.VMEM((ITERS, 8, SIDE), f32)
+    return (
+        [padded, padded, pltpu.VMEM((ITERS, PLANES, SIDE, SIDE), f32), planes]
+        + [padded, planes, tile]
+        + [tile, tile]
+        + [padded, planes, planes, padded, padded, planes]
+        + [table, table]
+    )
+
+
+def solver_state():
+    wide = PLANES * SIDE
+    return quad_state() * QUADS + [pltpu.VMEM((2, wide, wide), jnp.bfloat16)]
+
+
+def quad_parts(state):
+    even, odd, hist, t_s, vert, hori, hori_in, edge_r, edge_l, isd_s, inj_s, gnd_s, v_s, res_s, h_s, tail_s, link_s = state
+    f32 = jnp.float32
+    mid = tuple(slice(8 + 8 * k, 16 + 8 * k) for k in range(SIDE // 8))
+    low = tuple(slice(9 + 8 * k, 17 + 8 * k) for k in range(SIDE // 8))
+    upp = tuple(slice(7 + 8 * k, 15 + 8 * k) for k in range(SIDE // 8))
+    blocks = range(SIDE // 8)
+    lane = lanes_of((8, SIDE))
+    row8 = lax.broadcasted_iota(jnp.int32, (8, SIDE), 0)
+
+    def clear():
+        zero = jnp.zeros((8, SIDE), f32)
+        for pad in (even, odd, vert, isd_s, v_s, res_s):
+            for p in range(PLANES):
+                pad[p, 0:8, :] = zero
+                pad[p, 8 + SIDE:16 + SIDE, :] = zero
+
+    def refresh_edges(cur):
+        for k in blocks:
+            edge_r[EIGHTS[k], :] = roll(cur[0, mid[k], :], -1, 1)
+            edge_l[EIGHTS[k], :] = roll(cur[PLANES - 1, mid[k], :], 1, 1)
+
+    def operate(cur):
+        gammas, deltas = [None] * PLANES, [None] * PLANES
+        for k in blocks:
+            here = [cur[p, mid[k], :] for p in range(PLANES)]
+            out = [hori[p, EIGHTS[k], :] for p in range(PLANES)]
+            for p in (1, 2, 0, 3):
+                right = here[p + 1] if p < PLANES - 1 else edge_r[EIGHTS[k], :]
+                left = here[p - 1] if p else edge_l[EIGHTS[k], :]
+                back = out[p - 1] if p else hori_in[EIGHTS[k], :]
+                beside = vert[p, mid[k], :] * cur[p, low[k], :] + vert[p, upp[k], :] * cur[p, upp[k], :]
+                beside = beside + (out[p] * right + back * left)
+                t_s[p, EIGHTS[k], :] = beside
+                one, two = here[p] * here[p], here[p] * beside
+                gammas[p] = one if k == 0 else gammas[p] + one
+                deltas[p] = two if k == 0 else deltas[p] + two
+        return (gammas[0] + gammas[1]) + (gammas[2] + gammas[3]), (deltas[0] + deltas[1]) + (deltas[2] + deltas[3])
+
+    def down_sum(part):
+        for shift in (4, 2, 1):
+            part = part + roll(part, shift, 0)
+        return part
+
+    def total_of(sums):
+        mine = lane // SEGMENTS == row8 % PLANES
+        first = row8 < PLANES
+        both = jnp.where(first, down_sum(sums[0]), down_sum(sums[1]))
+        both = jnp.where(mine, jnp.sum(jnp.where(mine, both, 0.0), axis=1, keepdims=True), 0.0)
+        return down_sum(jnp.where(first, both, 0.0)), down_sum(jnp.where(first, 0.0, both))
+
+    def prepare(load, table):
+        for r in range(0, SIDE, CHUNK):
+            cut = slice(r, r + CHUNK)
+            loaded = [load(w, cut) for w in range(PLANES)]
+            res = jnp.concatenate([pair[0] for pair in loaded], axis=1)
+            mark = jnp.concatenate([pair[1] for pair in loaded], axis=1)
+            high, low_part, mark = mixed([*halves(res), mark.astype(jnp.bfloat16)], table)
+            res = high + low_part
+            signed = mark / res
+            for p in range(PLANES):
+                span = slice(SIDE * p, SIDE * p + SIDE)
+                res_s[p, 8 + r:8 + r + CHUNK, :] = res[:, span]
+                inject = jnp.maximum(signed[:, span], 0.0)
+                if p == 0 and r <= RAD < r + CHUNK:
+                    at = lax.broadcasted_iota(jnp.int32, (CHUNK, SIDE), 0) == RAD - r
+                    spot = lanes_of((CHUNK, SIDE)) % SEGMENTS == RAD // PLANES
+                    inject = inject + (at & spot).astype(f32)
+                inj_s[p, cut, :] = inject
+                gnd_s[p, cut, :] = jnp.maximum(-signed[:, span], 0.0)
+        ends = lane % SEGMENTS == SEGMENTS - 1
+        bottom = row8 == 7
+        for k in blocks:
+            for p in range(PLANES):
+                here = res_s[p, mid[k], :]
+                under = res_s[p, low[k], :]
+                if k == len(EIGHTS) - 1:
+                    vertical = jnp.where(bottom, 0.0, 2.0 / (here + jnp.where(bottom, FAR, under)))
+                else:
+                    vertical = 2.0 / (here + under)
+                v_s[p, mid[k], :] = vertical
+                if p < PLANES - 1:
+                    h_s[p, EIGHTS[k], :] = 2.0 / (here + res_s[p + 1, mid[k], :])
+                else:
+                    horizontal = jnp.where(ends, 0.0, 2.0 / (here + roll(res_s[0, mid[k], :], -1, 1)))
+                    h_s[p, EIGHTS[k], :] = horizontal
+                    edge_l[EIGHTS[k], :] = roll(horizontal, 1, 1)
+        for k in blocks:
+            for p in range(PLANES):
+                before = h_s[p - 1, EIGHTS[k], :] if p else edge_l[EIGHTS[k], :]
+                diagonal = v_s[p, mid[k], :] + v_s[p, upp[k], :] + (h_s[p, EIGHTS[k], :] + before)
+                isd_s[p, mid[k], :] = 1.0 / jnp.sqrt(diagonal + gnd_s[p, EIGHTS[k], :] + LEAKAGE)
+        for k in blocks:
+            for p in range(PLANES):
+                isd = isd_s[p, mid[k], :]
+                vert[p, mid[k], :] = v_s[p, mid[k], :] * isd * isd_s[p, low[k], :]
+                if p < PLANES - 1:
+                    hori[p, EIGHTS[k], :] = h_s[p, EIGHTS[k], :] * isd * isd_s[p + 1, mid[k], :]
+                else:
+                    scaled = h_s[p, EIGHTS[k], :] * isd * roll(isd_s[0, mid[k], :], -1, 1)
+                    hori[p, EIGHTS[k], :] = scaled
+                    hori_in[EIGHTS[k], :] = roll(scaled, 1, 1)
+                first = inj_s[p, EIGHTS[k], :] * isd
+                even[p, mid[k], :] = first
+                hist[0, p, EIGHTS[k], :] = first
+        refresh_edges(even)
+        return operate(even)
+
+    def settle(j, sums, gamma_inv_before, pivot_inv, weight):
+        gamma, delta = sums
+        gamma_inv = 1.0 / gamma
+        mean = delta * gamma_inv
+        ratio = gamma * gamma_inv_before
+        link = ratio * pivot_inv
+        pivot_inv = 1.0 / (1.0 - mean - link)
+        weight = weight * pivot_inv
+        tail_s[j] = weight
+        link_s[j] = link
+        return mean, ratio, gamma_inv, pivot_inv, weight
+
+    def update(j, way, mean, ratio):
+        cur, new = (odd, even) if way else (even, odd)
+        for p in (0, 3, 1, 2):
+            for k in blocks:
+                fresh = t_s[p, EIGHTS[k], :] - mean * cur[p, mid[k], :]
+                if ratio is not None:
+                    fresh = fresh - ratio * new[p, mid[k], :]
+                new[p, mid[k], :] = fresh
+                hist[j + 1, p, EIGHTS[k], :] = fresh
+                if p == 0:
+                    edge_r[EIGHTS[k], :] = roll(fresh, -1, 1)
+                if p == PLANES - 1:
+                    edge_l[EIGHTS[k], :] = roll(fresh, 1, 1)
+        return operate(new)
+
+    def coefficients():
+        factor = tail_s[ITERS - 1]
+        for j in reversed(range(1, ITERS)):
+            ahead = tail_s[j - 1] + link_s[j] * factor
+            tail_s[j] = factor
+            factor = ahead
+        tail_s[0] = factor
+
+    def voltages():
+        def one(p, _):
+            for half in range(2):
+                found = [None] * 8
+                for j in range(ITERS):
+                    factor = tail_s[j]
+                    for i in range(8):
+                        term = factor * hist[j, p, EIGHTS[8 * half + i], :]
+                        found[i] = term if found[i] is None else found[i] + term
+                for i in range(8):
+                    even[p, mid[8 * half + i], :] = found[i] * isd_s[p, mid[8 * half + i], :]
+            return 0
+
+        lax.fori_loop(0, PLANES, one, 0)
+
+    def finish(put, table):
+        cur = even
+        for k in blocks:
+            edge_r[EIGHTS[k], :] = roll(cur[0, mid[k], :], -1, 1)
+        for k in blocks:
+            for p in range(PLANES):
+                volts = cur[p, mid[k], :]
+                res_s[p, mid[k], :] = v_s[p, mid[k], :] * jnp.abs(volts - cur[p, low[k], :])
+                right = cur[p + 1, mid[k], :] if p < PLANES - 1 else edge_r[EIGHTS[k], :]
+                flow = h_s[p, EIGHTS[k], :] * jnp.abs(volts - right)
+                t_s[p, EIGHTS[k], :] = flow
+                if p == PLANES - 1:
+                    edge_l[EIGHTS[k], :] = roll(flow, 1, 1)
+
+        for r in range(0, SIDE, CHUNK):
+            cut = slice(r, r + CHUNK)
+            pieces = []
+            for p in range(PLANES):
+                flow = res_s[p, 8 + r:8 + r + CHUNK, :] + res_s[p, 7 + r:7 + r + CHUNK, :] + t_s[p, cut, :]
+                flow = flow + (t_s[p - 1, cut, :] if p else edge_l[cut, :])
+                pieces.append(0.5 * (flow + inj_s[p, cut, :] + gnd_s[p, cut, :] * jnp.abs(cur[p, 8 + r:8 + r + CHUNK, :])))
+            high, low_part = mixed(halves(jnp.concatenate(pieces, axis=1)), table)
+            for w in range(PLANES):
+                span = slice(SIDE * w, SIDE * w + SIDE)
+                put(w, cut, high[:, span] + low_part[:, span])
+
+    return clear, prepare, total_of, operate, settle, update, coefficients, voltages, finish
+
+
 def solver_parts(state):
-    r_s, p_s, s_s, x_s, w_s, vd_s, vu_s, hr_s, hl_s, isd_s, inj_s, gnd_s, v_s, h_s = state
-    row_id = lax.broadcasted_iota(jnp.int32, (SIDE, SIDE), 0)
-    col_id = lax.broadcasted_iota(jnp.int32, (SIDE, SIDE), 1)
-
-    def operate(b):
-        here = r_s[b, 8:8 + SIDE, :]
-        down = r_s[b, 9:9 + SIDE, :]
-        up = r_s[b, 7:7 + SIDE, :]
-        beside = vd_s[b] * down + vu_s[b] * up
-        beside = beside + hr_s[b] * roll(here, -1, 1) + hl_s[b] * roll(here, 1, 1)
-        applied = here - beside
-        w_s[b] = applied
-        return total(here * here), total(here * applied)
-
-    def prepare(b, res, signed):
-        res_down, res_right = roll(res, -1, 0), roll(res, -1, 1)
-        has_down = (res > 0.0) & (res_down > 0.0) & (row_id < SIDE - 1)
-        has_right = (res > 0.0) & (res_right > 0.0) & (col_id < SIDE - 1)
-        vertical = jnp.where(has_down, 2.0 / jnp.where(has_down, res + res_down, 1.0), 0.0)
-        horizontal = jnp.where(has_right, 2.0 / jnp.where(has_right, res + res_right, 1.0), 0.0)
-        center = ((row_id == RAD) & (col_id == RAD)).astype(jnp.float32)
-        inject = jnp.maximum(signed, 0.0) + center
-        ground = jnp.maximum(-signed, 0.0)
-        diagonal = vertical + roll(vertical, 1, 0) + horizontal + roll(horizontal, 1, 1) + ground + LEAKAGE
-        isd = 1.0 / jnp.sqrt(diagonal)
-        scaled_v = vertical * isd * roll(isd, -1, 0)
-        scaled_h = horizontal * isd * roll(isd, -1, 1)
-        v_s[b], h_s[b] = vertical, horizontal
-        vd_s[b], vu_s[b] = scaled_v, roll(scaled_v, 1, 0)
-        hr_s[b], hl_s[b] = scaled_h, roll(scaled_h, 1, 1)
-        inj_s[b], gnd_s[b], isd_s[b] = inject, ground, isd
-        r_s[b, 0:8, :] = jnp.zeros((8, SIDE), jnp.float32)
-        r_s[b, 8 + SIDE:16 + SIDE, :] = jnp.zeros((8, SIDE), jnp.float32)
-        r_s[b, 8:8 + SIDE, :] = inject * isd
-        zero = jnp.zeros((SIDE, SIDE), jnp.float32)
-        p_s[b], s_s[b], x_s[b] = zero, zero, zero
-
-    def step(_, carry):
-        after = []
-        for b in range(GROUP):
-            alpha, beta, _, _ = carry[b]
-            here = r_s[b, 8:8 + SIDE, :]
-            direction = here + beta * p_s[b]
-            applied = w_s[b] + beta * s_s[b]
-            p_s[b] = direction
-            s_s[b] = applied
-            x_s[b] = x_s[b] + alpha * direction
-            r_s[b, 8:8 + SIDE, :] = here - alpha * applied
-        for b in range(GROUP):
-            _, _, gamma_inv, alpha_inv = carry[b]
-            gamma, delta = operate(b)
-            beta = gamma * gamma_inv
-            bottom = delta - beta * (gamma * alpha_inv)
-            gamma_inv = 1.0 / gamma
-            after.append((gamma / bottom, beta, gamma_inv, bottom * gamma_inv))
-        return tuple(after)
-
-    def finish(b):
-        isd, vertical, horizontal = isd_s[b], v_s[b], h_s[b]
-        voltage = x_s[b] * isd
-        flow_down = vertical * jnp.abs(voltage - roll(voltage, -1, 0))
-        flow_right = horizontal * jnp.abs(voltage - roll(voltage, -1, 1))
-        flow = flow_down + roll(flow_down, 1, 0) + flow_right + roll(flow_right, 1, 1)
-        return 0.5 * (flow + inj_s[b] + gnd_s[b] * jnp.abs(voltage))
-
-    def iterate():
+    table = state[-1]
+    size = (len(state) - 1) // QUADS
+    quads = [quad_parts(state[size * q:size * q + size]) for q in range(QUADS)]
+
+    def clear():
+        for quad in quads:
+            quad[0]()
+        for way in range(2):
+            table[way] = interleave(table.shape[1:], way == 1)
+
+    def solve(load, store):
+        one = jnp.ones((8, SIDE), jnp.float32)
         carry = []
-        for b in range(GROUP):
-            gamma, delta = operate(b)
-            gamma_inv = 1.0 / gamma
-            carry.append((gamma / delta, jnp.zeros_like(gamma), gamma_inv, delta * gamma_inv))
-        lax.fori_loop(0, ITERS, step, tuple(carry))
-
-    return prepare, iterate, finish
+        for q, (_, prepare, total_of, *_) in enumerate(quads):
+            sums = prepare(lambda w, cut, q=q: load(PLANES * q + w, cut), table.at[0])
+            carry.append((sums if q else total_of(sums), 0.0 * one, 0.0 * one, one))
+
+        def step(j, way, carry, first=False):
+            after = []
+            for q, (_, _, total_of, operate, settle, update, *_) in enumerate(quads):
+                sums, *rest = carry[q]
+                if q:
+                    sums = total_of(sums)
+                mean, ratio, *rest = settle(j, sums, *rest)
+                sums = update(j, way, mean, None if first else ratio)
+                after.append((sums if q else total_of(sums), *rest))
+            return after
+
+        def steps(i, carry):
+            return tuple(step(2 * i + 2, 0, step(2 * i + 1, 1, carry)))
+
+        carry = tuple(step(0, 0, carry, True))
+        carry = lax.fori_loop(0, (ITERS - 2) // 2, steps, carry)
+        for q, (_, _, total_of, _, settle, _, coefficients, *_) in enumerate(quads):
+            settle(ITERS - 1, total_of(carry[q][0]) if q else carry[q][0], *carry[q][1:])
+            coefficients()
+        for q, (*_, voltages, finish) in enumerate(quads):
+            voltages()
+            finish(lambda w, cut, tile, q=q: store(PLANES * q + w, cut, tile), table.at[1])
+
+    return clear, solve
 
 
 def spans_of(rows, cols):
@@ -266,10 +471,16 @@
         top, left, row, col = place(slot)
         res, mark = turn_own(*(buf[slot] for buf in bufs), top - row, col - left)
         out[0, slot] = res
-        out[1, slot] = mark / res
+        out[1, slot] = mark
         return 0
 
+    def blank(slot, _):
+        out[0, slot] = jnp.ones((SIDE, SIDE), jnp.float32)
+        out[1, slot] = jnp.zeros((SIDE, SIDE), jnp.float32)
+        return 0
+
     lax.fori_loop(0, live[0], begin, 0)
+    lax.fori_loop(live[0], out.shape[1], blank, 0)
     lax.fori_loop(0, live[0], cut, 0)
 
 
@@ -279,9 +490,10 @@
     pieces, halos = dict(zip(SHIFTS, refs[12:20])), dict(zip(SHIFTS, refs[20:28]))
     frames = [refs[28 + 3 * k:31 + 3 * k] for k in range(4)]
     sems, send_sems, recv_sems = refs[40:43]
-    prepare, iterate, finish = solver_parts(refs[43:])
+    clear, solve = solver_parts(refs[43:])
     slots = windows.shape[1]
     found = neighbours()
+    clear()
 
     everything = pl.ds(0, rows)
     places = (
@@ -303,8 +515,7 @@
     def strengths(frame, cut=slice(None)):
         res, source, target = (ref[cut] for ref in frame)
         source, target = source.astype(jnp.float32), target.astype(jnp.float32)
-        conduct = 1.0 / res
-        return res, source * conduct - target * (1.0 - source) * conduct
+        return res, source - target * (1.0 - source)
 
     for f, at in enumerate(((0, -1), (0, 1), (-1, 0), (1, 0))):
         for copy in frame_copies[f]:
@@ -322,19 +533,13 @@
     start_all(copies)
 
     def solve_group(group, _):
-        def ready(b, _):
-            slot = group * GROUP + b
-            prepare(b, windows[0, slot], windows[1, slot])
-            return 0
-
-        lax.fori_loop(0, GROUP, ready, 0)
-        iterate()
-
-        def done(b, _):
-            cur[group * GROUP + b] = finish(b)
-            return 0
-
-        lax.fori_loop(0, GROUP, done, 0)
+        def load(b, cut):
+            return windows[0, group * GROUP + b, cut, :], windows[1, group * GROUP + b, cut, :]
+
+        def store(b, cut, current):
+            cur[group * GROUP + b, cut, :] = current
+
+        solve(load, store)
         return 0
 
     lax.fori_loop(0, slots // GROUP, solve_group, 0)
@@ -361,8 +566,8 @@
 def border_kernel(rows, cols, centers, live, inner_cur, *refs):
     raw, halos = refs[:3], dict(zip(SHIFTS, refs[3:11]))
     out, outs = refs[11], dict(zip(SHIFTS, refs[12:20]))
-    bufs, sems, order, ext, acc, out_sem = refs[20:23], *refs[23:28]
-    prepare, iterate, finish = solver_parts(refs[28:])
+    bufs, sems, order, ext, acc, out_sem, staged, solved = refs[20:23], *refs[23:30]
+    clear, solve = solver_parts(refs[30:])
 
     def copies(slot):
         top, left = corner_of(centers, slot, rows, cols)
@@ -390,6 +595,7 @@
 
     count = lax.fori_loop(0, live[0], classify, jnp.int32(0))
     acc[...] = jnp.zeros_like(acc)
+    clear()
     spans = spans_of(rows, cols)
     for which in range(2):
         for dr in (-1, 1):
@@ -421,8 +627,8 @@
             cut_rows(pltpu.roll(ext[k, span, pl.ds(base, WIDE)], back, 1)[:, :SIDE], lax.rem(top + RAD, 8))
             for k in range(2)
         ]
-        signed = jnp.where(own, mark / jnp.where(own, res, 1.0), outer[1])
-        return jnp.where(own, res, outer[0]), signed
+        res = jnp.where(own, res, outer[0])
+        return jnp.where(res > 0.0, res, FAR), jnp.where(own, mark, outer[1])
 
     def solve_group(group, _):
         def ready(b, _):
@@ -434,23 +640,20 @@
                 for copy in copies(slot):
                     copy.wait()
 
-            prepare(b, *fetch(slot))
+            staged[0, b], staged[1, b] = fetch(slot)
             return 0
 
+        def store(b, cut, current):
+            solved[b, cut, :] = current
+
+        def done(b, _):
+            top, left = corner_of(centers, order[group * GROUP + b], rows, cols)
+            add_window(acc, solved[b], top, left)
+            return 0
+
         lax.fori_loop(0, GROUP, ready, 0)
-        iterate()
-
-        def done(b, _):
-            at = group * GROUP + b
-
-            @pl.when(at < count)
-            def _():
-                top, left = corner_of(centers, order[at], rows, cols)
-                add_window(acc, finish(b), top, left)
-
-            return 0
-
-        lax.fori_loop(0, GROUP, done, 0)
+        solve(lambda b, cut: (staged[0, b, cut, :], staged[1, b, cut, :]), store)
+        lax.fori_loop(0, jnp.minimum(count - group * GROUP, GROUP), done, 0)
         return 0
 
     lax.fori_loop(0, (count + GROUP - 1) // GROUP, solve_group, 0)
@@ -532,7 +735,8 @@
     }
     pairs = [pltpu.VMEM((2, *shapes[at]), f32) for at in SHIFTS]
     strips = [pltpu.VMEM(shapes[at], f32) for at in SHIFTS]
-    state = [pltpu.VMEM((GROUP, SIDE + 16, SIDE), f32)] + [pltpu.VMEM((GROUP, SIDE, SIDE), f32)] * 13
+    state = solver_state()
+    stage = [pltpu.VMEM((2, GROUP, SIDE, SIDE), f32), pltpu.VMEM((GROUP, SIDE, SIDE), f32)]
     kinds = (f32, i32, i32)
     frame_shapes = ((rows, LANES), (rows, LANES), (RAD, cols), (RAD, cols))
 
@@ -576,8 +780,9 @@
             pltpu.VMEM((rows + SIDE, cols + WIDE), f32),
             pltpu.SemaphoreType.DMA,
         ]
+        + stage
         + state,
-        compiler_params=pltpu.CompilerParams(vmem_limit_bytes=45 << 20),
+        compiler_params=pltpu.CompilerParams(vmem_limit_bytes=58 << 20),
         name="border",
     )(centers, live_counts, inner_cur, resistance, source_mask, target_mask, *halos)
 

time: 99.6 us -> 93.1 us (0.935)
  Pallas kernels: 95.9 us -> 77.5 us
  local copies, waits for them, and re-layouts: 2.57 us -> 13.7 us
    pallas_call x1, Pallas kernels: 48.1 us -> 32.7 us  [local(): pl.pallas_call(functools.partial(inner_kernel, rows, cols), out_shape=[ja...]
    unnamed x7 -> x33, local copies, waits for them, and re-layouts: 2.57 us -> 13.7 us
    pallas_call x1, Pallas kernels: 29.6 us -> 21 us  [local(): pl.pallas_call(functools.partial(border_kernel, rows, cols), out_shape=[j...]
    pallas_call x1, Pallas kernels: 9.12 us -> 16.7 us  [local(): pl.pallas_call(return_kernel, out_shape=[jax.ShapeDtypeStruct(shapes[at],...]
    pallas_call x1, Pallas kernels: 6.39 us -> 4.47 us  [local(): pl.pallas_call(functools.partial(cut_kernel, rows, cols), out_shape=jax.S...]
where the time goes in v1:
time: 93.1 us; the launch traced here: 91.9 us
  Pallas kernels  77.5 us (83%)
  local copies, waits for them, and re-layouts  13.7 us (15%)
    pallas_call x1, Pallas kernels, local(): pl.pallas_call(functools.partial(inner_kernel, rows, cols), out_shape=[ja...  32.7 us
    pallas_call x1, Pallas kernels, local(): pl.pallas_call(functools.partial(border_kernel, rows, cols), out_shape=[j...  21 us
    pallas_call x1, Pallas kernels, local(): pl.pallas_call(return_kernel, out_shape=[jax.ShapeDtypeStruct(shapes[at],...  16.7 us
    unnamed x33, local copies, waits for them, and re-layouts  13.7 us
    pallas_call x1, Pallas kernels, local(): pl.pallas_call(functools.partial(cut_kernel, rows, cols), out_shape=jax.S...  4.47 us
    pallas_call x1, Pallas kernels, local(): pl.pallas_call(functools.partial(fold_kernel, rows, cols), out_shape=out_...  2.68 us

profile of v1, /device:TPU:0, one launch (start us, length us, event | category | flops | bytes accessed | tf_op | source)
XLA Modules:
  0.0 91.9 jit_solution(14976886842519424128)
XLA Ops:
  0.7 1.3 %copy.8.centers = s32[16,2]{1,0:T(8,128)} copy(s32[16,2]{0,1:T(2,128)} %param.8) | data formatting | bytes 256 | tf_op args[3]
  2.0 4.5 %cut.1.windows = f32[2,16,128,128]{3,2,1,0:T(8,128)} custom-call(s32[16,2]{1,0:T(8,128)} %copy.8.centers, s32[1]{0:T(128)S(6)} %copy.10.live, f32[1024,1024]{1,0:T(8,128)} %refs_0_.5, s32[1024,1024]{1,0:T(8,128)} %refs_1_.5, s32[1024,1024]{1,0:T(8,128)} %refs_2_.5), custom_call_target="tpu_custom_call" | custom-call | tf_op jit(solution)/shard_map/cut/pallas_call | solution.py:743
  6.5 32.7 %inner.1 = (f32[16,128,128]{2,1,0:T(8,128)}, f32[2,512,128]{2,1,0:T(8,128)S(1)}, f32[2,512,128]{2,1,0:T(8,128)S(1)}, f32[2,64,1024]{2,1,0:T(8,128)S(1)}, f32[2,6...) custom-call(f32[2,16,128,128]{3,2,1,0:T(8,128)} %cut.1.windows, ...), custom_call_target="tpu_custom_call" | custom-call | tf_op jit(solution)/shard_map/inner/pallas_call | solution.py:754
  39.1 0.0 copy-start
  39.1 0.8 copy-done
  40.0 0.0 copy-start.1
  40.0 0.8 copy-done.1
  40.8 0.0 copy-start.2
  40.8 0.8 copy-done.2
  41.6 0.0 copy-start.3
  41.6 0.8 copy-done.3
  42.4 0.0 copy-start.8
  42.4 0.6 copy-done.8
  43.0 0.0 copy-start.9
  43.0 0.6 copy-done.9
  43.6 0.0 copy-start.10
  43.6 0.6 copy-done.10
  44.2 0.0 copy-start.11
  44.2 0.6 copy-done.11
  44.8 21.0 %border.1 = (f32[1024,1024]{1,0:T(8,128)}, f32[512,128]{1,0:T(8,128)}, f32[512,128]{1,0:T(8,128)}, f32[64,1024]{1,0:T(8,128)}, f32[64,1024]{1,0:T(8,128)}, /*ind...) custom-call(s32[16,2]{1,0:T(8,128)} %copy.8.centers, s32[1]{0:T(128)S(6)} %copy.10.live, ...), custom_call_target="tpu_custom_call" | custom-call | tf_op jit(solution)/shard_map/border/pallas_call | solution.py:769
  65.8 0.0 copy-start.4
  65.9 0.9 %copy-done.4 = f32[512,128]{1,0:T(8,128)S(1)} copy-done((f32[512,128]{1,0:T(8,128)S(1)}, f32[512,128]{1,0:T(8,128)}, u32[]{:S(2)}) %copy-start.4) | copy-done | bytes 262168
  66.8 0.0 copy-start.5
  66.8 0.9 %copy-done.5 = f32[512,128]{1,0:T(8,128)S(1)} copy-done((f32[512,128]{1,0:T(8,128)S(1)}, f32[512,128]{1,0:T(8,128)}, u32[]{:S(2)}) %copy-start.5) | copy-done | bytes 262168
  67.8 0.0 copy-start.6
  67.8 0.9 %copy-done.6 = f32[64,1024]{1,0:T(8,128)S(1)} copy-done((f32[64,1024]{1,0:T(8,128)S(1)}, f32[64,1024]{1,0:T(8,128)}, u32[]{:S(2)}) %copy-start.6) | copy-done | bytes 262168
  68.7 0.0 copy-start.7
  68.7 0.9 %copy-done.7 = f32[64,1024]{1,0:T(8,128)S(1)} copy-done((f32[64,1024]{1,0:T(8,128)S(1)}, f32[64,1024]{1,0:T(8,128)}, u32[]{:S(2)}) %copy-start.7) | copy-done | bytes 262168
  69.7 0.0 copy-start.12
  69.7 0.7 copy-done.12
  70.4 0.0 copy-start.13
  70.4 0.7 copy-done.13
  71.1 0.0 copy-start.14
  71.1 0.7 copy-done.14
  71.8 0.0 copy-start.15
  71.8 0.7 copy-done.15
  72.5 16.7 %give_back.1 = (f32[512,128]{1,0:T(8,128)S(1)}, f32[512,128]{1,0:T(8,128)S(1)}, f32[64,1024]{1,0:T(8,128)S(1)}, f32[64,1024]{1,0:T(8,128)S(1)}, f32[32,128]{1,0:...) custom-call(f32[512,128]{1,0:T(8,128)S(1)} %copy-done.4, ...), custom_call_target="tpu_custom_call" | custom-call | tf_op jit(solution)/shard_map/give_back/pallas_call | solution.py:789
  89.2 2.7 %fold.1 = f32[1024,1024]{1,0:T(8,128)} custom-call(f32[1024,1024]{1,0:T(8,128)} %get-tuple-element.40.refs_0_, f32[512,128]{1,0:T(8,128)S(1)} %get-tuple-element.49.refs_1_, f32[512,128]{1,0:T(8,128)S(1)} %get-tuple-element.50.refs_2_, f32[64,1024]{1,0:T(8,128)S(1)} %get-tuple-element.51.refs_3_, ...), custom_call_target="tpu_custom_call", output_to_operand_aliasing={{}: (0, {})} | custom-call | tf_op jit(solution)/shard_map/fold/pallas_call | solution.py:800
Async XLA Ops:
  39.1 0.8 copy-start
  40.0 0.8 copy-start.1
  40.8 0.8 copy-start.2
  41.6 0.8 copy-start.3
  42.4 0.6 copy-start.8
  43.0 0.6 copy-start.9
  43.6 0.6 copy-start.10
  44.2 0.6 copy-start.11
  65.8 1.0 %copy-start.4 = (f32[512,128]{1,0:T(8,128)S(1)}, f32[512,128]{1,0:T(8,128)}, u32[]{:S(2)}) copy-start(f32[512,128]{1,0:T(8,128)} %get-tuple-element.41.refs_0_) | copy-start | bytes 786436
  66.8 0.9 %copy-start.5 = (f32[512,128]{1,0:T(8,128)S(1)}, f32[512,128]{1,0:T(8,128)}, u32[]{:S(2)}) copy-start(f32[512,128]{1,0:T(8,128)} %get-tuple-element.42.refs_1_) | copy-start | bytes 786436
  67.8 0.9 %copy-start.6 = (f32[64,1024]{1,0:T(8,128)S(1)}, f32[64,1024]{1,0:T(8,128)}, u32[]{:S(2)}) copy-start(f32[64,1024]{1,0:T(8,128)} %get-tuple-element.43.refs_2_) | copy-start | bytes 786436
  68.7 0.9 %copy-start.7 = (f32[64,1024]{1,0:T(8,128)S(1)}, f32[64,1024]{1,0:T(8,128)}, u32[]{:S(2)}) copy-start(f32[64,1024]{1,0:T(8,128)} %get-tuple-element.44.refs_3_) | copy-start | bytes 786436
  69.7 0.7 copy-start.12
  70.4 0.7 copy-start.13
  71.1 0.7 copy-start.14
  71.8 0.7 copy-start.15

commit v2 on v1

--- a/solution.py
+++ b/solution.py
@@ -12,8 +12,7 @@
 ITERS = 24
 LEAKAGE = 0.02
 FAR = 1e37
-QUADS = 2
-GROUP = 4 * QUADS
+GROUP = 8
 LANES = 128
 TALL = SIDE + 8
 WIDE = 2 * LANES
@@ -193,9 +192,9 @@
     )
 
 
-def solver_state():
+def solver_state(group):
     wide = PLANES * SIDE
-    return quad_state() * QUADS + [pltpu.VMEM((2, wide, wide), jnp.bfloat16)]
+    return quad_state() * (group // PLANES) + [pltpu.VMEM((2, wide, wide), jnp.bfloat16)]
 
 
 def quad_parts(state):
@@ -385,10 +384,11 @@
     return clear, prepare, total_of, operate, settle, update, coefficients, voltages, finish
 
 
-def solver_parts(state):
+def solver_parts(state, group):
     table = state[-1]
-    size = (len(state) - 1) // QUADS
-    quads = [quad_parts(state[size * q:size * q + size]) for q in range(QUADS)]
+    count = group // PLANES
+    size = (len(state) - 1) // count
+    quads = [quad_parts(state[size * q:size * q + size]) for q in range(count)]
 
     def clear():
         for quad in quads:
@@ -490,7 +490,7 @@
     pieces, halos = dict(zip(SHIFTS, refs[12:20])), dict(zip(SHIFTS, refs[20:28]))
     frames = [refs[28 + 3 * k:31 + 3 * k] for k in range(4)]
     sems, send_sems, recv_sems = refs[40:43]
-    clear, solve = solver_parts(refs[43:])
+    clear, solve = solver_parts(refs[43:], GROUP)
     slots = windows.shape[1]
     found = neighbours()
     clear()
@@ -567,16 +567,16 @@
     raw, halos = refs[:3], dict(zip(SHIFTS, refs[3:11]))
     out, outs = refs[11], dict(zip(SHIFTS, refs[12:20]))
     bufs, sems, order, ext, acc, out_sem, staged, solved = refs[20:23], *refs[23:30]
-    clear, solve = solver_parts(refs[30:])
-
-    def copies(slot):
+    clear, solve = solver_parts(refs[30:], PLANES)
+
+    def copies(slot, at):
         top, left = corner_of(centers, slot, rows, cols)
         row, col = clamped(top, left, rows, cols)
         return [
             pltpu.make_async_copy(
                 src.at[pl.ds(row, TALL), pl.ds(col, WIDE)],
-                dst.at[slot, pl.ds(RAD, TALL), :],
-                sems.at[k, slot],
+                dst.at[at, pl.ds(RAD, TALL), :],
+                sems.at[k, at],
             )
             for k, (src, dst) in enumerate(zip(raw, bufs))
         ]
@@ -588,8 +588,6 @@
         @pl.when(outer)
         def _():
             order[count] = slot
-            for copy in copies(slot):
-                copy.start()
 
         return count + outer.astype(jnp.int32)
 
@@ -612,11 +610,11 @@
     row_id = lax.broadcasted_iota(jnp.int32, (SIDE, SIDE), 0)
     col_id = lax.broadcasted_iota(jnp.int32, (SIDE, SIDE), 1)
 
-    def fetch(slot):
+    def fetch(slot, b):
         top, left = corner_of(centers, slot, rows, cols)
         row, col = clamped(top, left, rows, cols)
         take = pl.ds(pl.multiple_of((RAD + top - row) // 8 * 8, 8), TALL)
-        res, source, target = (buf[slot, take, :] for buf in bufs)
+        res, source, target = (buf[b, take, :] for buf in bufs)
         res, mark = turn_own(res, source, target, lax.rem(RAD + top - row, 8), col - left)
         at_row, at_col = row_id + top, col_id + left
         own = (at_row >= 0) & (at_row < rows) & (at_col >= 0) & (at_col < cols)
@@ -631,32 +629,40 @@
         return jnp.where(res > 0.0, res, FAR), jnp.where(own, mark, outer[1])
 
     def solve_group(group, _):
+        size = jnp.minimum(count - group * PLANES, PLANES)
+
+        def begin(b, _):
+            for copy in copies(order[group * PLANES + b], b):
+                copy.start()
+            return 0
+
         def ready(b, _):
-            at = group * GROUP + b
-            slot = order[jnp.minimum(at, count - 1)]
-
-            @pl.when(at < count)
+            b_own = jnp.minimum(b, size - 1)
+            slot = order[group * PLANES + b_own]
+
+            @pl.when(b < size)
             def _():
-                for copy in copies(slot):
+                for copy in copies(slot, b):
                     copy.wait()
 
-            staged[0, b], staged[1, b] = fetch(slot)
+            staged[0, b], staged[1, b] = fetch(slot, b_own)
             return 0
 
         def store(b, cut, current):
             solved[b, cut, :] = current
 
         def done(b, _):
-            top, left = corner_of(centers, order[group * GROUP + b], rows, cols)
+            top, left = corner_of(centers, order[group * PLANES + b], rows, cols)
             add_window(acc, solved[b], top, left)
             return 0
 
-        lax.fori_loop(0, GROUP, ready, 0)
+        lax.fori_loop(0, size, begin, 0)
+        lax.fori_loop(0, PLANES, ready, 0)
         solve(lambda b, cut: (staged[0, b, cut, :], staged[1, b, cut, :]), store)
-        lax.fori_loop(0, jnp.minimum(count - group * GROUP, GROUP), done, 0)
+        lax.fori_loop(0, size, done, 0)
         return 0
 
-    lax.fori_loop(0, (count + GROUP - 1) // GROUP, solve_group, 0)
+    lax.fori_loop(0, (count + PLANES - 1) // PLANES, solve_group, 0)
 
     def place(slot, _):
         top, left = corner_of(centers, slot, rows, cols)
@@ -735,8 +741,7 @@
     }
     pairs = [pltpu.VMEM((2, *shapes[at]), f32) for at in SHIFTS]
     strips = [pltpu.VMEM(shapes[at], f32) for at in SHIFTS]
-    state = solver_state()
-    stage = [pltpu.VMEM((2, GROUP, SIDE, SIDE), f32), pltpu.VMEM((GROUP, SIDE, SIDE), f32)]
+    stage = [pltpu.VMEM((2, PLANES, SIDE, SIDE), f32), pltpu.VMEM((PLANES, SIDE, SIDE), f32)]
     kinds = (f32, i32, i32)
     frame_shapes = ((rows, LANES), (rows, LANES), (RAD, cols), (RAD, cols))
 
@@ -761,8 +766,8 @@
         + pairs
         + [pltpu.VMEM(shape, kind) for shape in frame_shapes for kind in kinds]
         + [pltpu.SemaphoreType.DMA((4, 3)), pltpu.SemaphoreType.DMA((8,)), pltpu.SemaphoreType.DMA((8,))]
-        + state,
-        compiler_params=pltpu.CompilerParams(vmem_limit_bytes=51 << 20, collective_id=0, has_side_effects=True),
+        + solver_state(GROUP),
+        compiler_params=pltpu.CompilerParams(vmem_limit_bytes=46 << 20, collective_id=0, has_side_effects=True),
         name="inner",
     )(windows, resistance, source_mask, target_mask)
 
@@ -772,17 +777,17 @@
         + [jax.ShapeDtypeStruct(shapes[at], f32) for at in SHIFTS],
         in_specs=[smem, smem, vmem, hbm, hbm, hbm] + [vmem] * 8,
         out_specs=[hbm] + [vmem] * 8,
-        scratch_shapes=[pltpu.VMEM((slots, TALL + SIDE, WIDE), kind) for kind in kinds]
+        scratch_shapes=[pltpu.VMEM((PLANES, TALL + SIDE, WIDE), kind) for kind in kinds]
         + [
-            pltpu.SemaphoreType.DMA((3, slots)),
+            pltpu.SemaphoreType.DMA((3, PLANES)),
             pltpu.SMEM((slots,), i32),
             pltpu.VMEM((2, rows + SIDE, cols + WIDE), f32),
             pltpu.VMEM((rows + SIDE, cols + WIDE), f32),
             pltpu.SemaphoreType.DMA,
         ]
         + stage
-        + state,
-        compiler_params=pltpu.CompilerParams(vmem_limit_bytes=58 << 20),
+        + solver_state(PLANES),
+        compiler_params=pltpu.CompilerParams(vmem_limit_bytes=42 << 20),
         name="border",
     )(centers, live_counts, inner_cur, resistance, source_mask, target_mask, *halos)
 

time: 93.1 us -> 82.6 us (0.89)
  the two profiles are of different devices: /device:TPU:0 before, /device:TPU:18 now
where the time goes in v2:
time: 82.6 us; the launch traced here: 81.1 us
  Pallas kernels  77.4 us (94%)
  local copies, waits for them, and re-layouts  2.94 us (4%)
    pallas_call x1, Pallas kernels, local(): pl.pallas_call(functools.partial(inner_kernel, rows, cols), out_shape=[ja...  29.8 us
    pallas_call x1, Pallas kernels, local(): pl.pallas_call(return_kernel, out_shape=[jax.ShapeDtypeStruct(shapes[at],...  26.9 us
    pallas_call x1, Pallas kernels, local(): pl.pallas_call(functools.partial(border_kernel, rows, cols), out_shape=[j...  14.2 us
    pallas_call x1, Pallas kernels, local(): pl.pallas_call(functools.partial(cut_kernel, rows, cols), out_shape=jax.S...  3.76 us
    unnamed x7, local copies, waits for them, and re-layouts  2.94 us
    pallas_call x1, Pallas kernels, local(): pl.pallas_call(functools.partial(fold_kernel, rows, cols), out_shape=out_...  2.68 us

profile of v2, /device:TPU:18, one launch (start us, length us, event | category | flops | bytes accessed | tf_op | source)
XLA Modules:
  0.0 81.1 jit_solution(3294000786040858327)
XLA Ops:
  0.7 1.4 %copy.8.centers = s32[16,2]{1,0:T(8,128)} copy(s32[16,2]{0,1:T(2,128)} %param.8) | data formatting | bytes 256 | tf_op args[3]
  2.0 3.8 %cut.1.windows = f32[2,16,128,128]{3,2,1,0:T(8,128)} custom-call(s32[16,2]{1,0:T(8,128)} %copy.8.centers, s32[1]{0:T(128)S(6)} %copy.10.live, f32[1024,1024]{1,0:T(8,128)} %refs_0_.5, s32[1024,1024]{1,0:T(8,128)} %refs_1_.5, s32[1024,1024]{1,0:T(8,128)} %refs_2_.5), custom_call_target="tpu_custom_call" | custom-call | tf_op jit(solution)/shard_map/cut/pallas_call | solution.py:748
  5.8 0.0 copy-start.1
  5.8 1.6 %copy-done.1 = f32[2,16,128,128]{3,2,1,0:T(8,128)S(1)} copy-done((f32[2,16,128,128]{3,2,1,0:T(8,128)S(1)}, f32[2,16,128,128]{3,2,1,0:T(8,128)}, u32[]{:S(2)}) %copy-start.1) | copy-done | bytes 2097176
  7.4 0.0 copy-start
  7.4 0.0 copy-start.2
  7.4 29.8 %inner.1 = (f32[16,128,128]{2,1,0:T(8,128)S(1)}, f32[2,512,128]{2,1,0:T(8,128)S(1)}, f32[2,512,128]{2,1,0:T(8,128)S(1)}, f32[2,64,1024]{2,1,0:T(8,128)S(1)}, f32...) custom-call(f32[2,16,128,128]{3,2,1,0:T(8,128)S(1)} %copy-done.1, ...), custom_call_target="tpu_custom_call" | custom-call | tf_op jit(solution)/shard_map/inner/pallas_call | solution.py:759
  37.2 0.0 copy-done
  37.2 0.0 copy-done.2
  37.2 14.2 %border.1 = (f32[1024,1024]{1,0:T(8,128)}, f32[512,128]{1,0:T(8,128)S(1)}, f32[512,128]{1,0:T(8,128)S(1)}, f32[64,1024]{1,0:T(8,128)S(1)}, f32[64,1024]{1,0:T(8,...) custom-call(s32[16,2]{1,0:T(8,128)S(1)} %copy-done.2, ...), custom_call_target="tpu_custom_call" | custom-call | tf_op jit(solution)/shard_map/border/pallas_call | solution.py:774
  51.5 26.9 %give_back.1 = (f32[512,128]{1,0:T(8,128)S(1)}, f32[512,128]{1,0:T(8,128)S(1)}, f32[64,1024]{1,0:T(8,128)S(1)}, f32[64,1024]{1,0:T(8,128)S(1)}, f32[32,128]{1,0:...) custom-call(f32[512,128]{1,0:T(8,128)S(1)} %get-tuple-element.41.refs_0_, ...), custom_call_target="tpu_custom_call" | custom-call | tf_op jit(solution)/shard_map/give_back/pallas_call | solution.py:794
  78.4 2.7 %fold.1 = f32[1024,1024]{1,0:T(8,128)} custom-call(f32[1024,1024]{1,0:T(8,128)} %get-tuple-element.40.refs_0_, f32[512,128]{1,0:T(8,128)S(1)} %get-tuple-element.49.refs_1_, f32[512,128]{1,0:T(8,128)S(1)} %get-tuple-element.50.refs_2_, f32[64,1024]{1,0:T(8,128)S(1)} %get-tuple-element.51.refs_3_, ...), custom_call_target="tpu_custom_call", output_to_operand_aliasing={{}: (0, {})} | custom-call | tf_op jit(solution)/shard_map/fold/pallas_call | solution.py:805
Async XLA Ops:
  5.8 1.6 %copy-start.1 = (f32[2,16,128,128]{3,2,1,0:T(8,128)S(1)}, f32[2,16,128,128]{3,2,1,0:T(8,128)}, u32[]{:S(2)}) copy-start(f32[2,16,128,128]{3,2,1,0:T(8,128)} %cut.1.windows) | copy-start | bytes 6291460
  7.4 29.8 %copy-start = (f32[1024,1024]{1,0:T(8,128)S(1)}, f32[1024,1024]{1,0:T(8,128)}, u32[]{:S(2)}) copy-start(f32[1024,1024]{1,0:T(8,128)} %refs_0_.5) | copy-start | bytes 12582916
  7.4 29.8 %copy-start.2 = (s32[16,2]{1,0:T(8,128)S(1)}, s32[16,2]{1,0:T(8,128)}, u32[]{:S(2)}) copy-start(s32[16,2]{1,0:T(8,128)} %copy.8.centers) | copy-start | bytes 388

commit v3 on v2

--- a/solution.py
+++ b/solution.py
@@ -72,9 +72,10 @@
     pl.semaphore_wait(pltpu.get_barrier_semaphore(), count)
 
 
-def transfers(found, pieces, halos, send_sems, recv_sems):
+def transfers(found, pieces, halos, send_sems, recv_sems, ats=SHIFTS):
     made = []
-    for k, at in enumerate(SHIFTS):
+    for at in ats:
+        k = SHIFTS.index(at)
         exists, device = found[at]
         back = (-at[0], -at[1])
         made.append((exists, pltpu.make_async_remote_copy(
@@ -88,9 +89,10 @@
     return made
 
 
-def landings(found, pieces, halos, send_sems, recv_sems):
+def landings(found, pieces, halos, send_sems, recv_sems, ats=SHIFTS):
     made = []
-    for k, at in enumerate(SHIFTS):
+    for at in ats:
+        k = SHIFTS.index(at)
         exists, device = found[at]
         made.append((exists, pltpu.make_async_remote_copy(
             src_ref=pieces[at],
@@ -116,7 +118,7 @@
 
 
 def corner_of(centers, slot, rows, cols):
-    return lax.rem(centers[slot, 0], rows) - RAD, lax.rem(centers[slot, 1], cols) - RAD
+    return lax.rem(centers[0, slot], rows) - RAD, lax.rem(centers[1, slot], cols) - RAD
 
 
 def is_inner(top, left, rows, cols):
@@ -437,6 +439,11 @@
     }
 
 
+def mark_of(source, target):
+    source, target = source.astype(jnp.float32), target.astype(jnp.float32)
+    return source - target * (1.0 - source)
+
+
 def turn_own(res, source, target, skip, turn):
     source, target = source.astype(jnp.float32), target.astype(jnp.float32)
     mark = source - target * (1.0 - source)
@@ -446,54 +453,13 @@
     return res, mark
 
 
-def cut_kernel(rows, cols, centers, live, *refs):
-    raw, out, bufs, sems = refs[:3], refs[3], refs[4:7], refs[7]
-
-    def place(slot):
-        top, left = corner_of(centers, slot, rows, cols)
-        return top, left, *clamped(top, left, rows, cols)
-
-    def copies(slot):
-        _, _, row, col = place(slot)
-        return [
-            pltpu.make_async_copy(src.at[pl.ds(row, TALL), pl.ds(col, WIDE)], dst.at[slot], sems.at[k, slot])
-            for k, (src, dst) in enumerate(zip(raw, bufs))
-        ]
-
-    def begin(slot, _):
-        for copy in copies(slot):
-            copy.start()
-        return 0
-
-    def cut(slot, _):
-        for copy in copies(slot):
-            copy.wait()
-        top, left, row, col = place(slot)
-        res, mark = turn_own(*(buf[slot] for buf in bufs), top - row, col - left)
-        out[0, slot] = res
-        out[1, slot] = mark
-        return 0
-
-    def blank(slot, _):
-        out[0, slot] = jnp.ones((SIDE, SIDE), jnp.float32)
-        out[1, slot] = jnp.zeros((SIDE, SIDE), jnp.float32)
-        return 0
-
-    lax.fori_loop(0, live[0], begin, 0)
-    lax.fori_loop(live[0], out.shape[1], blank, 0)
-    lax.fori_loop(0, live[0], cut, 0)
-
-
-def inner_kernel(rows, cols, windows, *refs):
+def strips_kernel(rows, cols, *refs):
     raw = refs[:3]
-    cur, outs = refs[3], dict(zip(SHIFTS, refs[4:12]))
-    pieces, halos = dict(zip(SHIFTS, refs[12:20])), dict(zip(SHIFTS, refs[20:28]))
-    frames = [refs[28 + 3 * k:31 + 3 * k] for k in range(4)]
-    sems, send_sems, recv_sems = refs[40:43]
-    clear, solve = solver_parts(refs[43:], GROUP)
-    slots = windows.shape[1]
+    outs = dict(zip(SHIFTS, refs[3:11]))
+    pieces, halos = dict(zip(SHIFTS, refs[11:19])), dict(zip(SHIFTS, refs[19:27]))
+    frames = [refs[27 + 3 * k:30 + 3 * k] for k in range(4)]
+    sems, send_sems, recv_sems = refs[39:42]
     found = neighbours()
-    clear()
 
     everything = pl.ds(0, rows)
     places = (
@@ -532,17 +498,6 @@
     copies = transfers(found, pieces, halos, send_sems, recv_sems)
     start_all(copies)
 
-    def solve_group(group, _):
-        def load(b, cut):
-            return windows[0, group * GROUP + b, cut, :], windows[1, group * GROUP + b, cut, :]
-
-        def store(b, cut, current):
-            cur[group * GROUP + b, cut, :] = current
-
-        solve(load, store)
-        return 0
-
-    lax.fori_loop(0, slots // GROUP, solve_group, 0)
     finish_all(copies, landings(found, pieces, halos, send_sems, recv_sems))
     for at in SHIFTS:
         outs[at][...] = halos[at][...]
@@ -563,11 +518,11 @@
         outs[at][...] = halos[at][...]
 
 
-def border_kernel(rows, cols, centers, live, inner_cur, *refs):
+def border_kernel(rows, cols, centers, live, *refs):
     raw, halos = refs[:3], dict(zip(SHIFTS, refs[3:11]))
     out, outs = refs[11], dict(zip(SHIFTS, refs[12:20]))
-    bufs, sems, order, ext, acc, out_sem, staged, solved = refs[20:23], *refs[23:30]
-    clear, solve = solver_parts(refs[30:], PLANES)
+    bufs, sems, ext, acc, out_sem, staged, solved = refs[20:23], *refs[23:29]
+    clear, solve = solver_parts(refs[29:], PLANES)
 
     def copies(slot, at):
         top, left = corner_of(centers, slot, rows, cols)
@@ -581,17 +536,7 @@
             for k, (src, dst) in enumerate(zip(raw, bufs))
         ]
 
-    def classify(slot, count):
-        top, left = corner_of(centers, slot, rows, cols)
-        outer = jnp.logical_not(is_inner(top, left, rows, cols))
-
-        @pl.when(outer)
-        def _():
-            order[count] = slot
-
-        return count + outer.astype(jnp.int32)
-
-    count = lax.fori_loop(0, live[0], classify, jnp.int32(0))
+    count = live[0]
     acc[...] = jnp.zeros_like(acc)
     clear()
     spans = spans_of(rows, cols)
@@ -632,13 +577,13 @@
         size = jnp.minimum(count - group * PLANES, PLANES)
 
         def begin(b, _):
-            for copy in copies(order[group * PLANES + b], b):
+            for copy in copies((group * PLANES + b), b):
                 copy.start()
             return 0
 
         def ready(b, _):
             b_own = jnp.minimum(b, size - 1)
-            slot = order[group * PLANES + b_own]
+            slot = (group * PLANES + b_own)
 
             @pl.when(b < size)
             def _():
@@ -652,7 +597,7 @@
             solved[b, cut, :] = current
 
         def done(b, _):
-            top, left = corner_of(centers, order[group * PLANES + b], rows, cols)
+            top, left = corner_of(centers, (group * PLANES + b), rows, cols)
             add_window(acc, solved[b], top, left)
             return 0
 
@@ -664,16 +609,6 @@
 
     lax.fori_loop(0, (count + PLANES - 1) // PLANES, solve_group, 0)
 
-    def place(slot, _):
-        top, left = corner_of(centers, slot, rows, cols)
-
-        @pl.when(is_inner(top, left, rows, cols))
-        def _():
-            add_window(acc, inner_cur[slot], top, left)
-
-        return 0
-
-    lax.fori_loop(0, live[0], place, 0)
     copy = pltpu.make_async_copy(acc.at[pl.ds(RAD, rows), pl.ds(LANES, cols)], out, out_sem)
     copy.start()
     for dr in (-1, 1):
@@ -728,14 +663,445 @@
         copy.wait()
 
 
-def local(resistance, source_mask, target_mask, centers, live_counts):
-    rows, cols = resistance.shape
-    slots = centers.shape[0]
+MAIN = SHIFTS[:4]
+PIECES = 4
+
+
+def wait_for(found, ats, peers):
+    count = sum(found[at][0].astype(jnp.int32) for at in ats) + len(peers)
+    pl.semaphore_wait(pltpu.get_barrier_semaphore(), count)
+
+
+def hello(found, ats, peers):
+    barrier = pltpu.get_barrier_semaphore()
+    for at in ats:
+        exists, device = found[at]
+
+        @pl.when(exists)
+        def _():
+            pl.semaphore_signal(barrier, inc=1, device_id=device, device_id_type=pl.DeviceIdType.MESH)
+
+    for device in peers:
+        pl.semaphore_signal(barrier, inc=1, device_id=device, device_id_type=pl.DeviceIdType.MESH)
+
+
+def peers_along(axis):
+    row, col = lax.axis_index("row"), lax.axis_index("col")
+    size = lax.axis_size(axis)
+    if axis == "row":
+        return [(lax.rem(row + k, size), col) for k in range(1, size)]
+    return [(row, lax.rem(col + k, size)) for k in range(1, size)]
+
+
+def share_flag(flag, landed, peers, send_sems, recv_sems):
+    return [
+        pltpu.make_async_remote_copy(
+            src_ref=flag, dst_ref=landed.at[k], send_sem=send_sems.at[k], recv_sem=recv_sems.at[k],
+            device_id=device, device_id_type=pl.DeviceIdType.MESH,
+        )
+        for k, device in enumerate(peers)
+    ]
+
+
+def largest(flag, landed, peers):
+    found = flag[...]
+    for k in range(len(peers)):
+        found = jnp.maximum(found, landed[k])
+    return found
+
+
+def meta_kernel(centers, live, out, mine, halos, send_sems, recv_sems):
+    found = neighbours()
+    halos[...] = jnp.zeros_like(halos)
+    hello(found, MAIN, [])
+    slots = centers.shape[1]
+    row8 = lax.broadcasted_iota(jnp.int32, (8, LANES), 0)
+    lane8 = lanes_of((8, LANES))
+    block = jnp.broadcast_to(live[0], (8, LANES)).astype(jnp.int32)
+    for s in range(slots):
+        for axis in range(2):
+            block = jnp.where((row8 == axis) & (lane8 == s), centers[axis, s], block)
+    mine[...] = block
+    wait_for(found, MAIN, [])
+    args = (found, {at: mine for at in MAIN}, {at: halos.at[k] for k, at in enumerate(MAIN)}, send_sems, recv_sems)
+    copies = transfers(*args, ats=MAIN)
+    start_all(copies)
+    finish_all(copies, landings(*args, ats=MAIN))
+    out[...] = halos[...]
+
+
+def crosses(at, top, left, rows, cols):
+    tests = {(0, -1): left < 0, (0, 1): left + SIDE > cols, (-1, 0): top < 0, (1, 0): top + SIDE > rows}
+    return tests[at]
+
+
+def spot_of(at, row_of, col_of, slot, rows, cols):
+    return lax.rem(row_of(slot), rows) - RAD, lax.rem(col_of(slot), cols) - RAD
+
+
+def pack_kernel(rows, cols, centers, live, meta, *refs):
+    raw, windows, order = refs[:3], refs[3], refs[4]
+    pieces, flag = dict(zip(SHIFTS, refs[5:13])), refs[13]
+    bufs, piece_bufs, corner_bufs, sems, piece_sems, corner_sems = refs[14:17], refs[17:20], refs[20:23], *refs[23:26]
+    slots = centers.shape[1]
+    found = neighbours()
+
+    def corner(slot):
+        return lax.rem(centers[0, slot], rows) - RAD, lax.rem(centers[1, slot], cols) - RAD
+
+    def place(slot):
+        top, left = corner(slot)
+        return top, left, *clamped(top, left, rows, cols)
+
+    def copies(slot):
+        _, _, row, col = place(slot)
+        return [
+            pltpu.make_async_copy(src.at[pl.ds(row, TALL), pl.ds(col, WIDE)], dst.at[slot], sems.at[k, slot])
+            for k, (src, dst) in enumerate(zip(raw, bufs))
+        ]
+
+    def classify(slot, carry):
+        inner, outer, crossing = carry
+        for copy in copies(slot):
+            copy.start()
+        top, left = corner(slot)
+        inside = is_inner(top, left, rows, cols)
+        at = jnp.where(inside, inner, slots - 1 - outer)
+        order[0, at] = slot
+        step = inside.astype(jnp.int32)
+        fresh = []
+        for d, way in enumerate(MAIN):
+            over = crosses(way, top, left, rows, cols) & found[way][0]
+            order[2 + d, slot] = jnp.minimum(crossing[d], PIECES - 1)
+            fresh.append(crossing[d] + over.astype(jnp.int32))
+        return inner + step, outer + 1 - step, tuple(fresh)
+
+    zero = jnp.int32(0)
+    inner, outer, crossing = lax.fori_loop(0, live[0], classify, (zero, zero, (zero,) * 4))
+    order[1, 0] = inner
+    most = jnp.maximum(jnp.maximum(crossing[0], crossing[1]), jnp.maximum(crossing[2], crossing[3]))
+    flag[...] = jnp.broadcast_to((most > PIECES).astype(jnp.int32), flag.shape)
+
+    corners = []
+    for n, at in enumerate(SHIFTS[4:]):
+        r = pl.ds(0 if at[0] < 0 else rows - RAD, RAD)
+        c = pl.ds(0 if at[1] < 0 else cols - LANES, LANES)
+        corners += [
+            pltpu.make_async_copy(src.at[r, c], dst.at[n], corner_sems.at[k, n])
+            for k, (src, dst) in enumerate(zip(raw, corner_bufs))
+        ]
+    for copy in corners:
+        copy.start()
+
+    def theirs(d, slot):
+        return lax.rem(meta[d, 0, slot], rows) - RAD, lax.rem(meta[d, 1, slot], cols) - RAD
+
+    def piece_place(d, k):
+        at = MAIN[d]
+        top, left = theirs(d, order[6 + d, k])
+        if at[1]:
+            row = pl.multiple_of(jnp.clip((top + RAD) // 8 * 8 - RAD, 0, rows - TALL), 8)
+            return row, 0 if at[1] < 0 else cols - LANES, top - row
+        col = pl.multiple_of(jnp.clip((left + LANES) // LANES * LANES - LANES, 0, cols - WIDE), LANES)
+        return 0 if at[0] < 0 else rows - RAD, col, left - col
+
+    def piece_copies(d, k):
+        row, col, _ = piece_place(d, k)
+        size = (TALL, LANES) if MAIN[d][1] else (RAD, WIDE)
+        return [
+            pltpu.make_async_copy(
+                src.at[pl.ds(row, size[0]), pl.ds(col, size[1])],
+                dst.at[d, k, pl.ds(0, size[0]), pl.ds(0, size[1])],
+                piece_sems.at[n, d, k],
+            )
+            for n, (src, dst) in enumerate(zip(raw, piece_bufs))
+        ]
+
+    counts = []
+    for d, at in enumerate(MAIN):
+        back = (-at[0], -at[1])
+
+        def look(slot, count, d=d, back=back):
+            top, left = theirs(d, slot)
+            hit = crosses(back, top, left, rows, cols)
+
+            @pl.when(hit & (count < PIECES))
+            def _():
+                order[6 + d, count] = slot
+                for copy in piece_copies(d, count):
+                    copy.start()
+
+            return count + hit.astype(jnp.int32)
+
+        limit = jnp.where(found[at][0], meta[d, 2, 0], 0)
+        count = jnp.minimum(lax.fori_loop(0, limit, look, zero), PIECES)
+        order[1, 1 + d] = count
+        counts.append(count)
+
+    def blank(slot, _):
+        windows[0, slot] = jnp.ones((SIDE, SIDE), jnp.float32)
+        windows[1, slot] = jnp.zeros((SIDE, SIDE), jnp.float32)
+        return 0
+
+    def cut(n, _):
+        at = jnp.where(n < inner, n, slots - 1 - (n - inner))
+        slot = order[0, at]
+        for copy in copies(slot):
+            copy.wait()
+        top, left, row, col = place(slot)
+        res, mark = turn_own(*(buf[slot] for buf in bufs), top - row, col - left)
+        windows[0, at] = res
+        windows[1, at] = mark
+        return 0
+
+    lax.fori_loop(inner, slots - outer, blank, 0)
+    lax.fori_loop(0, live[0], cut, 0)
+    for n, at in enumerate(SHIFTS[4:]):
+        for k in range(3):
+            corners[3 * n + k].wait()
+        squeeze = pack_low if at[1] < 0 else pack_high
+        res, source, target = (buf[n] for buf in corner_bufs)
+        pieces[at][0] = squeeze(res)
+        pieces[at][1] = squeeze(mark_of(source, target))
+    for d, at in enumerate(MAIN):
+        def fill(k, _, d=d, at=at):
+            for copy in piece_copies(d, k):
+                copy.wait()
+            _, _, skip = piece_place(d, k)
+            if at[1]:
+                res, source, target = (buf[d, k, :, 0:LANES] for buf in piece_bufs)
+                squeeze = pack_low if at[1] < 0 else pack_high
+                pieces[at][0, k] = squeeze(cut_rows(res, skip))
+                pieces[at][1, k] = squeeze(cut_rows(mark_of(source, target), skip))
+            else:
+                res, source, target = (buf[d, k, 0:RAD, :] for buf in piece_bufs)
+                turn = lax.rem(2 * WIDE - skip, WIDE)
+                pieces[at][0, k] = pltpu.roll(res, turn, 1)[:, :SIDE]
+                pieces[at][1, k] = pltpu.roll(mark_of(source, target), turn, 1)[:, :SIDE]
+            return 0
+
+        lax.fori_loop(0, counts[d], fill, 0)
+
+
+def trade_kernel(windows, flag, *refs):
+    pieces = dict(zip(SHIFTS, refs[:8]))
+    cur, outs, flag_out = refs[8], dict(zip(SHIFTS, refs[9:17])), refs[17]
+    halos = dict(zip(SHIFTS, refs[18:26]))
+    flag_landed, send_sems, recv_sems, flag_send, flag_recv = refs[26:31]
+    clear, solve = solver_parts(refs[31:], GROUP)
+    found = neighbours()
+    peers = peers_along("row")
+    for at in SHIFTS:
+        halos[at][...] = jnp.zeros_like(halos[at])
+    hello(found, SHIFTS, peers)
+    wait_for(found, SHIFTS, peers)
+    copies = transfers(found, pieces, halos, send_sems, recv_sems)
+    start_all(copies)
+    shared = share_flag(flag, flag_landed, peers, flag_send, flag_recv)
+    for copy in shared:
+        copy.start()
+    clear()
+
+    def store(b, cut, current):
+        cur[b, cut, :] = current
+
+    solve(lambda b, cut: (windows[0, b, cut, :], windows[1, b, cut, :]), store)
+    for copy in shared:
+        copy.wait()
+    flag_out[...] = largest(flag, flag_landed, peers)
+    finish_all(copies, landings(found, pieces, halos, send_sems, recv_sems))
+    for at in SHIFTS:
+        outs[at][...] = halos[at][...]
+
+
+def unpacked(packed, dc):
+    return jnp.concatenate((to_high if dc < 0 else to_low)(packed), axis=0)
+
+
+def rest_kernel(rows, cols, centers, live, order, windows, inner_cur, *refs):
+    halos, out, outs = dict(zip(SHIFTS, refs[:8])), refs[8], dict(zip(SHIFTS, refs[9:17]))
+    acc, out_sem, staged, solved = refs[17:21]
+    clear, solve = solver_parts(refs[21:], GROUP)
+    slots = centers.shape[1]
+    inner = order[1, 0]
+    ready_count = jnp.minimum(inner, GROUP)
+    acc[...] = jnp.zeros_like(acc)
+    clear()
+    row_id = lax.broadcasted_iota(jnp.int32, (SIDE, SIDE), 0)
+    col_id = lax.broadcasted_iota(jnp.int32, (SIDE, SIDE), 1)
+    blank = jnp.zeros((RAD, SIDE), jnp.float32)
+
+    def corner(slot):
+        return lax.rem(centers[0, slot], rows) - RAD, lax.rem(centers[1, slot], cols) - RAD
+
+    def seat(n):
+        return jnp.where(n < inner, n, slots - 1 - (n - inner))
+
+    def place(n, _):
+        top, left = corner(order[0, n])
+        add_window(acc, inner_cur[n], top, left)
+        return 0
+
+    lax.fori_loop(0, ready_count, place, 0)
+
+    def shifts(top, left):
+        down = {-1: -top, 1: rows - top, 0: None}
+        side = {-1: -left, 1: cols - left, 0: None}
+        return down, side
+
+    def ranges(at, top, left):
+        at_row, at_col = row_id + top, col_id + left
+        row_ok = {-1: at_row < 0, 0: (at_row >= 0) & (at_row < rows), 1: at_row >= rows}[at[0]]
+        col_ok = {-1: at_col < 0, 0: (at_col >= 0) & (at_col < cols), 1: at_col >= cols}[at[1]]
+        return row_ok & col_ok
+
+    def concerns(at, top, left):
+        hit = None
+        for way in ((at[0], 0), (0, at[1])):
+            if way != (0, 0):
+                one = crosses(way, top, left, rows, cols)
+                hit = one if hit is None else hit & one
+        return hit
+
+    def patch(b, slot):
+        top, left = corner(slot)
+        down, side = shifts(top, left)
+        for d, at in enumerate(SHIFTS):
+            @pl.when(concerns(at, top, left))
+            def _():
+                mask = ranges(at, top, left)
+                for k in range(2):
+                    if at[0] and at[1]:
+                        tile = unpacked(halos[at][k], at[1])
+                        tile = jnp.concatenate((blank, tile) if at[0] < 0 else (tile, blank), axis=0)
+                    elif at[1]:
+                        tile = unpacked(halos[at][k, order[2 + d, slot]], at[1])
+                    else:
+                        tile = halos[at][k, order[2 + d, slot]]
+                        tile = jnp.concatenate((blank, tile) if at[0] < 0 else (tile, blank), axis=0)
+                    if at[1]:
+                        tile = pltpu.roll(tile, side[at[1]], 1)
+                    if at[0]:
+                        tile = pltpu.roll(tile, down[at[0]], 0)
+                    staged[k, b] = jnp.where(mask, tile, staged[k, b])
+
+        res = staged[0, b]
+        staged[0, b] = jnp.where(res > 0.0, res, FAR)
+
+    def give(b, slot):
+        top, left = corner(slot)
+        down, side = shifts(top, left)
+        for d, at in enumerate(MAIN):
+            @pl.when(concerns(at, top, left))
+            def _():
+                tile = jnp.where(ranges(at, top, left), solved[b], 0.0)
+                if at[1]:
+                    tile = pltpu.roll(tile, lax.rem(2 * SIDE - side[at[1]], SIDE), 1)
+                    outs[at][order[2 + d, slot]] = (pack_high if at[1] < 0 else pack_low)(tile)
+                else:
+                    tile = pltpu.roll(tile, lax.rem(2 * SIDE - down[at[0]], SIDE), 0)
+                    outs[at][order[2 + d, slot]] = tile[RAD:] if at[0] < 0 else tile[:RAD]
+
+    def solve_group(group, _):
+        first = ready_count + group * GROUP
+        size = jnp.minimum(live[0] - first, GROUP)
+
+        def ready(b, _):
+            n = seat(first + jnp.minimum(b, size - 1))
+            staged[0, b] = windows[0, n]
+            staged[1, b] = windows[1, n]
+            patch(b, order[0, n])
+            return 0
+
+        def store(b, cut, current):
+            solved[b, cut, :] = current
+
+        def done(b, _):
+            slot = order[0, seat(first + b)]
+            top, left = corner(slot)
+            add_window(acc, solved[b], top, left)
+            give(b, slot)
+            return 0
+
+        lax.fori_loop(0, GROUP, ready, 0)
+        solve(lambda b, cut: (staged[0, b, cut, :], staged[1, b, cut, :]), store)
+        lax.fori_loop(0, size, done, 0)
+        return 0
+
+    lax.fori_loop(0, (live[0] - ready_count + GROUP - 1) // GROUP, solve_group, 0)
+    copy = pltpu.make_async_copy(acc.at[pl.ds(RAD, rows), pl.ds(LANES, cols)], out, out_sem)
+    copy.start()
+    spans = spans_of(rows, cols)
+    for dr, dc in SHIFTS[4:]:
+        tile = acc[spans[dr][0], spans[dc][1]]
+        outs[(dr, dc)][...] = pack_high(tile) if dc < 0 else pack_low(tile)
+    copy.wait()
+
+
+def reply_kernel(flag, *refs):
+    pieces, outs, flag_out = dict(zip(SHIFTS, refs[:8])), dict(zip(SHIFTS, refs[8:16])), refs[16]
+    halos = dict(zip(SHIFTS, refs[17:25]))
+    flag_landed, send_sems, recv_sems, flag_send, flag_recv = refs[25:]
+    found = neighbours()
+    peers = peers_along("col")
+    for at in SHIFTS:
+        halos[at][...] = jnp.zeros_like(halos[at])
+    hello(found, SHIFTS, peers)
+    wait_for(found, SHIFTS, peers)
+    copies = transfers(found, pieces, halos, send_sems, recv_sems)
+    start_all(copies)
+    shared = share_flag(flag, flag_landed, peers, flag_send, flag_recv)
+    for copy in shared:
+        copy.start()
+    for copy in shared:
+        copy.wait()
+    flag_out[...] = largest(flag, flag_landed, peers)
+    finish_all(copies, landings(found, pieces, halos, send_sems, recv_sems))
+    for at in SHIFTS:
+        outs[at][...] = halos[at][...]
+
+
+def settle_kernel(rows, cols, meta, order, *refs):
+    halos = dict(zip(SHIFTS, refs[1:9]))
+    out, acc, out_sem = refs[9], refs[10], refs[11]
+    fetch = pltpu.make_async_copy(out, acc.at[pl.ds(RAD, rows), pl.ds(LANES, cols)], out_sem)
+    fetch.start()
+    fetch.wait()
+    blank = jnp.zeros((RAD, SIDE), jnp.float32)
+    for d, at in enumerate(MAIN):
+        def add(k, _, d=d, at=at):
+            slot = order[6 + d, k]
+            top = lax.rem(meta[d, 0, slot], rows) - RAD
+            left = lax.rem(meta[d, 1, slot], cols) - RAD
+            if at[1]:
+                first, second = (to_low if at[1] < 0 else to_high)(halos[at][k])
+                tile = jnp.concatenate((first, second), axis=0)
+                low = lanes_of(tile.shape) < RAD
+                tile = jnp.where(low if at[1] < 0 else jnp.logical_not(low), tile, 0.0)
+                add_window(acc, tile, top, 0 if at[1] < 0 else cols - LANES)
+            else:
+                tile = jnp.concatenate((halos[at][k], blank) if at[0] < 0 else (blank, halos[at][k]), axis=0)
+                add_window(acc, tile, 0 if at[0] < 0 else rows - SIDE, left)
+            return 0
+
+        lax.fori_loop(0, order[1, 1 + d], add, 0)
+    for dr, dc in SHIFTS[4:]:
+        first, second = (to_low if dc < 0 else to_high)(halos[(dr, dc)][...])
+        low = lanes_of(first.shape) < RAD
+        keep = low if dc < 0 else jnp.logical_not(low)
+        r = RAD if dr < 0 else rows
+        c = LANES if dc < 0 else cols
+        for n, part in enumerate((first, second)):
+            span = slice(r + RAD // 2 * n, r + RAD // 2 * n + RAD // 2), slice(c, c + LANES)
+            acc[span] = acc[span] + jnp.where(keep, part, 0.0)
+    store = pltpu.make_async_copy(acc.at[pl.ds(RAD, rows), pl.ds(LANES, cols)], out, out_sem)
+    store.start()
+    store.wait()
+
+
+def slow_path(rows, cols, centers, live, raster):
     f32, i32 = jnp.float32, jnp.int32
-    smem = pl.BlockSpec(memory_space=pltpu.SMEM)
-    vmem = pl.BlockSpec(memory_space=pltpu.VMEM)
-    hbm = pl.BlockSpec(memory_space=pltpu.HBM)
-
+    smem, vmem, hbm = (pl.BlockSpec(memory_space=m) for m in (pltpu.SMEM, pltpu.VMEM, pltpu.HBM))
     shapes = {
         at: (RAD if at[0] else rows, cols) if at[1] == 0 else ((RAD if at[0] else rows) // 2, LANES) for at in SHIFTS
     }
@@ -744,43 +1110,27 @@
     stage = [pltpu.VMEM((2, PLANES, SIDE, SIDE), f32), pltpu.VMEM((PLANES, SIDE, SIDE), f32)]
     kinds = (f32, i32, i32)
     frame_shapes = ((rows, LANES), (rows, LANES), (RAD, cols), (RAD, cols))
-
-    windows = pl.pallas_call(
-        functools.partial(cut_kernel, rows, cols),
-        out_shape=jax.ShapeDtypeStruct((2, slots, SIDE, SIDE), f32),
-        in_specs=[smem, smem, hbm, hbm, hbm],
-        out_specs=vmem,
-        scratch_shapes=[pltpu.VMEM((slots, TALL, WIDE), kind) for kind in kinds]
-        + [pltpu.SemaphoreType.DMA((3, slots))],
-        compiler_params=pltpu.CompilerParams(vmem_limit_bytes=57 << 20),
-        name="cut",
-    )(centers, live_counts, resistance, source_mask, target_mask)
-
-    inner_cur, *halos = pl.pallas_call(
-        functools.partial(inner_kernel, rows, cols),
-        out_shape=[jax.ShapeDtypeStruct((slots, SIDE, SIDE), f32)]
-        + [jax.ShapeDtypeStruct((2, *shapes[at]), f32) for at in SHIFTS],
-        in_specs=[vmem, hbm, hbm, hbm],
-        out_specs=[vmem] * 9,
+    halos = pl.pallas_call(
+        functools.partial(strips_kernel, rows, cols),
+        out_shape=[jax.ShapeDtypeStruct((2, *shapes[at]), f32) for at in SHIFTS],
+        in_specs=[hbm] * 3,
+        out_specs=[vmem] * 8,
         scratch_shapes=pairs
         + pairs
         + [pltpu.VMEM(shape, kind) for shape in frame_shapes for kind in kinds]
-        + [pltpu.SemaphoreType.DMA((4, 3)), pltpu.SemaphoreType.DMA((8,)), pltpu.SemaphoreType.DMA((8,))]
-        + solver_state(GROUP),
-        compiler_params=pltpu.CompilerParams(vmem_limit_bytes=46 << 20, collective_id=0, has_side_effects=True),
-        name="inner",
-    )(windows, resistance, source_mask, target_mask)
-
+        + [pltpu.SemaphoreType.DMA((4, 3)), pltpu.SemaphoreType.DMA((8,)), pltpu.SemaphoreType.DMA((8,))],
+        compiler_params=pltpu.CompilerParams(vmem_limit_bytes=24 << 20, collective_id=3, has_side_effects=True),
+        name="strips",
+    )(*raster)
     merged, *currents = pl.pallas_call(
         functools.partial(border_kernel, rows, cols),
         out_shape=[jax.ShapeDtypeStruct((rows, cols), f32)]
         + [jax.ShapeDtypeStruct(shapes[at], f32) for at in SHIFTS],
-        in_specs=[smem, smem, vmem, hbm, hbm, hbm] + [vmem] * 8,
+        in_specs=[smem, smem, hbm, hbm, hbm] + [vmem] * 8,
         out_specs=[hbm] + [vmem] * 8,
         scratch_shapes=[pltpu.VMEM((PLANES, TALL + SIDE, WIDE), kind) for kind in kinds]
         + [
             pltpu.SemaphoreType.DMA((3, PLANES)),
-            pltpu.SMEM((slots,), i32),
             pltpu.VMEM((2, rows + SIDE, cols + WIDE), f32),
             pltpu.VMEM((rows + SIDE, cols + WIDE), f32),
             pltpu.SemaphoreType.DMA,
@@ -789,22 +1139,19 @@
         + solver_state(PLANES),
         compiler_params=pltpu.CompilerParams(vmem_limit_bytes=42 << 20),
         name="border",
-    )(centers, live_counts, inner_cur, resistance, source_mask, target_mask, *halos)
-
+    )(centers, live, *raster, *halos)
     back = pl.pallas_call(
         return_kernel,
         out_shape=[jax.ShapeDtypeStruct(shapes[at], f32) for at in SHIFTS],
         in_specs=[vmem] * 8,
         out_specs=[vmem] * 8,
         scratch_shapes=strips + [pltpu.SemaphoreType.DMA((8,)), pltpu.SemaphoreType.DMA((8,))],
-        compiler_params=pltpu.CompilerParams(vmem_limit_bytes=8 << 20, collective_id=1, has_side_effects=True),
+        compiler_params=pltpu.CompilerParams(vmem_limit_bytes=8 << 20, collective_id=4, has_side_effects=True),
         name="give_back",
     )(*currents)
-    out_shape = jax.ShapeDtypeStruct((rows, cols), f32)
-
     return pl.pallas_call(
         functools.partial(fold_kernel, rows, cols),
-        out_shape=out_shape,
+        out_shape=jax.ShapeDtypeStruct((rows, cols), f32),
         in_specs=[hbm] + [vmem] * 8,
         out_specs=hbm,
         scratch_shapes=[
@@ -818,6 +1165,100 @@
         compiler_params=pltpu.CompilerParams(vmem_limit_bytes=16 << 20),
         name="fold",
     )(merged, *back)
+
+
+def local(resistance, source_mask, target_mask, centers, live):
+    rows, cols = resistance.shape
+    raster = (resistance, source_mask, target_mask)
+    centers = centers.T
+    slots = centers.shape[1]
+    f32, i32 = jnp.float32, jnp.int32
+    smem, vmem, hbm = (pl.BlockSpec(memory_space=m) for m in (pltpu.SMEM, pltpu.VMEM, pltpu.HBM))
+    dma = pltpu.SemaphoreType.DMA
+    kinds = (f32, i32, i32)
+    piece = {at: (RAD // 2, LANES) if at[0] and at[1] else (PIECES, RAD, LANES) for at in SHIFTS}
+    twice = [(2, *piece[at]) for at in SHIFTS]
+    flag_shape = jax.ShapeDtypeStruct((8, LANES), i32)
+    row_peers, col_peers = lax.axis_size("row") - 1, lax.axis_size("col") - 1
+
+    meta = pl.pallas_call(
+        meta_kernel,
+        out_shape=jax.ShapeDtypeStruct((len(MAIN), 8, LANES), i32),
+        in_specs=[smem, smem],
+        out_specs=vmem,
+        scratch_shapes=[pltpu.VMEM((8, LANES), i32), pltpu.VMEM((len(MAIN), 8, LANES), i32), dma((8,)), dma((8,))],
+        compiler_params=pltpu.CompilerParams(vmem_limit_bytes=1 << 20, collective_id=0, has_side_effects=True),
+        name="meta",
+    )(centers, live)
+
+    windows, order, *rest = pl.pallas_call(
+        functools.partial(pack_kernel, rows, cols),
+        out_shape=[jax.ShapeDtypeStruct((2, slots, SIDE, SIDE), f32), jax.ShapeDtypeStruct((10, slots), i32)]
+        + [jax.ShapeDtypeStruct(shape, f32) for shape in twice]
+        + [flag_shape],
+        in_specs=[smem, smem, smem, hbm, hbm, hbm],
+        out_specs=[vmem, smem] + [vmem] * 9,
+        scratch_shapes=[pltpu.VMEM((slots, TALL, WIDE), kind) for kind in kinds]
+        + [pltpu.VMEM((len(MAIN), PIECES, TALL, WIDE), kind) for kind in kinds]
+        + [pltpu.VMEM((4, RAD, LANES), kind) for kind in kinds]
+        + [dma((3, slots)), dma((3, len(MAIN), PIECES)), dma((3, 4))],
+        compiler_params=pltpu.CompilerParams(vmem_limit_bytes=40 << 20),
+        name="pack",
+    )(centers, live, meta, *raster)
+    pieces, flag = rest[:8], rest[8]
+
+    inner_cur, *rest = pl.pallas_call(
+        trade_kernel,
+        out_shape=[jax.ShapeDtypeStruct((GROUP, SIDE, SIDE), f32)]
+        + [jax.ShapeDtypeStruct(shape, f32) for shape in twice]
+        + [flag_shape],
+        in_specs=[vmem] * 10,
+        out_specs=[vmem] * 10,
+        scratch_shapes=[pltpu.VMEM(shape, f32) for shape in twice]
+        + [pltpu.VMEM((row_peers, 8, LANES), i32), dma((8,)), dma((8,)), dma((row_peers,)), dma((row_peers,))]
+        + solver_state(GROUP),
+        compiler_params=pltpu.CompilerParams(vmem_limit_bytes=32 << 20, collective_id=1, has_side_effects=True),
+        name="trade",
+    )(windows, flag, *pieces)
+    halos, flag = rest[:8], rest[8]
+
+    merged, *pieces = pl.pallas_call(
+        functools.partial(rest_kernel, rows, cols),
+        out_shape=[jax.ShapeDtypeStruct((rows, cols), f32)]
+        + [jax.ShapeDtypeStruct(piece[at], f32) for at in SHIFTS],
+        in_specs=[smem, smem, smem] + [vmem] * 10,
+        out_specs=[hbm] + [vmem] * 8,
+        scratch_shapes=[pltpu.VMEM((rows + SIDE, cols + WIDE), f32), dma]
+        + [pltpu.VMEM((2, GROUP, SIDE, SIDE), f32), pltpu.VMEM((GROUP, SIDE, SIDE), f32)]
+        + solver_state(GROUP),
+        compiler_params=pltpu.CompilerParams(vmem_limit_bytes=40 << 20),
+        name="rest",
+    )(centers, live, order, windows, inner_cur, *halos)
+
+    *halos, flag = pl.pallas_call(
+        reply_kernel,
+        out_shape=[jax.ShapeDtypeStruct(piece[at], f32) for at in SHIFTS] + [flag_shape],
+        in_specs=[vmem] * 9,
+        out_specs=[vmem] * 9,
+        scratch_shapes=[pltpu.VMEM(piece[at], f32) for at in SHIFTS]
+        + [pltpu.VMEM((col_peers, 8, LANES), i32), dma((8,)), dma((8,)), dma((col_peers,)), dma((col_peers,))],
+        compiler_params=pltpu.CompilerParams(vmem_limit_bytes=8 << 20, collective_id=2, has_side_effects=True),
+        name="reply",
+    )(flag, *pieces)
+
+    def quick():
+        return pl.pallas_call(
+            functools.partial(settle_kernel, rows, cols),
+            out_shape=jax.ShapeDtypeStruct((rows, cols), f32),
+            in_specs=[smem, smem, hbm] + [vmem] * 8,
+            out_specs=hbm,
+            scratch_shapes=[pltpu.VMEM((rows + SIDE, cols + WIDE), f32), dma],
+            input_output_aliases={2: 0},
+            compiler_params=pltpu.CompilerParams(vmem_limit_bytes=16 << 20),
+            name="settle",
+        )(meta, order, merged, *halos)
+
+    return lax.cond(flag[0, 0] > 0, lambda: slow_path(rows, cols, centers, live, raster), quick)
 
 
 def solution(mesh):

time: 82.6 us -> 66.8 us (0.81)
  the two profiles are of different devices: /device:TPU:18 before, /device:TPU:0 now
where the time goes in v3:
time: 66.8 us; the launch traced here: 66.5 us
  Pallas kernels  64.2 us (96%)
  between operations  1.5 us (2%)
    pallas_call x1, Pallas kernels, local(): pl.pallas_call(trade_kernel, out_shape=[jax.ShapeDtypeStruct((GROUP, SIDE...  16.7 us
    pallas_call x1, Pallas kernels, local(): pl.pallas_call(functools.partial(rest_kernel, rows, cols), out_shape=[jax...  15.5 us
    pallas_call x1, Pallas kernels, local(): pl.pallas_call(reply_kernel, out_shape=[jax.ShapeDtypeStruct(piece[at], f...  14.2 us
    pallas_call x1, Pallas kernels, local(): pl.pallas_call(meta_kernel, out_shape=jax.ShapeDtypeStruct((len(MAIN), 8,...  6.97 us
    pallas_call x1, Pallas kernels, local(): pl.pallas_call(functools.partial(pack_kernel, rows, cols), out_shape=[jax...  5.57 us
    pallas_call x1, Pallas kernels, quick(): pl.pallas_call(functools.partial(settle_kernel, rows, cols), out_shape=ja...  5.23 us

profile of v3, /device:TPU:0, one launch (start us, length us, event | category | flops | bytes accessed | tf_op | source)
XLA Modules:
  0.0 66.5 jit_solution(16872921001604315310)
XLA Ops:
  0.7 7.0 %meta.1 = s32[4,8,128]{2,1,0:T(8,128)S(1)} custom-call(s32[2,16]{1,0:T(2,128)} %bitcast.2, s32[1]{0:T(128)S(6)} %copy.14.live), custom_call_target="tpu_custom_call" | custom-call | tf_op jit(solution)/shard_map/meta/pallas_call | solution.py:1184
  7.6 0.0 copy-start.3
  7.6 0.0 copy-start.1
  7.7 0.0 copy-start.2
  7.7 5.6 %pack.1 = (f32[2,16,128,128]{3,2,1,0:T(8,128)S(1)}, s32[10,16]{1,0:T(8,128)S(1)}, f32[2,4,64,128]{3,2,1,0:T(8,128)S(1)}, f32[2,4,64,128]{3,2,1,0:T(8,128)S(1)}, ...) custom-call(s32[2,16]{1,0:T(2,128)} %bitcast.3, ...), custom_call_target="tpu_custom_call" | custom-call | tf_op jit(solution)/shard_map/pack/pallas_call | solution.py:1194
  13.2 0.0 copy-start
  13.3 16.7 %trade.1 = (f32[8,128,128]{2,1,0:T(8,128)S(1)}, f32[2,4,64,128]{3,2,1,0:T(8,128)S(1)}, f32[2,4,64,128]{3,2,1,0:T(8,128)S(1)}, f32[2,4,64,128]{3,2,1,0:T(8,128)S(...) custom-call(f32[2,16,128,128]{3,2,1,0:T(8,128)S(1)} %get-tuple-eleme, ...), custom_call_target="tpu_custom_call" | custom-call | tf_op jit(solution)/shard_map/trade/pallas_call | solution.py:1210
  29.9 0.0 copy-done.3
  29.9 15.5 %rest.1 = (f32[1024,1024]{1,0:T(8,128)}, f32[4,64,128]{2,1,0:T(8,128)S(1)}, f32[4,64,128]{2,1,0:T(8,128)S(1)}, f32[4,64,128]{2,1,0:T(8,128)S(1)}, f32[4,64,128]{...) custom-call(s32[2,16]{1,0:T(2,128)S(1)} %bitcast.4, ...), custom_call_target="tpu_custom_call" | custom-call | tf_op jit(solution)/shard_map/rest/pallas_call | solution.py:1225
  45.5 14.2 %reply.1 = (f32[4,64,128]{2,1,0:T(8,128)S(1)}, f32[4,64,128]{2,1,0:T(8,128)S(1)}, f32[4,64,128]{2,1,0:T(8,128)S(1)}, f32[4,64,128]{2,1,0:T(8,128)S(1)}, f32[32,1...) custom-call(s32[8,128]{1,0:T(8,128)S(1)} %get-tuple-element.130.flag, ...), custom_call_target="tpu_custom_call" | custom-call | tf_op jit(solution)/shard_map/reply/pallas_call | solution.py:1238
  59.7 0.5 slice.3
  60.8 0.0 copy-done.1
  60.8 0.0 copy-done.2
  60.8 0.0 copy-done
  60.8 5.5 %conditional.1 = (f32[1024,1024]{1,0:T(8,128)}) conditional(s32[]{:T(128)} %bitcast.1, (s32[4,8,128]{2,1,0:T(8,128)S(1)}, s32[10,16]{1,0:T(8,128)S(1)}, f32[1024,1024]{1,0:T(8,128)}, f32[4,64,128]{2,1,0:T(8,128)S(1)}, f32[4,64,128]{2,1,0:T(8,128)S(1)}, /*index=5*/f32[4,64,128]{2,1,0:T(8,128)S(1)}, f32[4,64,128]{2,1,0:T(8,128)S(1)}, ...), branch_computations={%region_0.0_spmd, %region_1.0_spmd} | conditional | bytes 8 | solution.py:1261
  60.8 5.2 %settle.1 = f32[1024,1024]{1,0:T(8,128)} custom-call(s32[4,8,128]{2,1,0:T(8,128)S(1)} %get-tuple-element.40.meta, s32[10,16]{1,0:T(8,128)S(1)} %get-tuple-element.41.order, f32[1024,1024]{1,0:T(8,128)} %get-tuple-element.42.refs_0_, f32[4,64,128]{2,1,0:T(8,128)S(1)} %get-tuple-element.43.refs_1_, ...), custom_call_target="tpu_custom_call", output_to_operand_aliasing={{}: (2, {})} | custom-call | tf_op jit(solution)/shard_map/cond/branch_0_fun/settle/pallas_call | solution.py:1250
Async XLA Ops:
  7.6 22.3 %copy-start.3 = (s32[16,2]{0,1:T(2,128)S(1)}, s32[16,2]{0,1:T(2,128)}, u32[]{:S(2)}) copy-start(s32[16,2]{0,1:T(2,128)} %param.10) | copy-start | bytes 388
  7.6 53.2 %copy-start.1 = (s32[1024,1024]{1,0:T(8,128)S(1)}, s32[1024,1024]{1,0:T(8,128)}, u32[]{:S(2)}) copy-start(s32[1024,1024]{1,0:T(8,128)} %refs_1_.1) | copy-start | bytes 12582916
  7.7 53.2 %copy-start.2 = (s32[1024,1024]{1,0:T(8,128)S(1)}, s32[1024,1024]{1,0:T(8,128)}, u32[]{:S(2)}) copy-start(s32[1024,1024]{1,0:T(8,128)} %refs_2_.1) | copy-start | bytes 12582916
  13.2 47.6 %copy-start = (f32[1024,1024]{1,0:T(8,128)S(1)}, f32[1024,1024]{1,0:T(8,128)}, u32[]{:S(2)}) copy-start(f32[1024,1024]{1,0:T(8,128)} %refs_0_.1) | copy-start | bytes 12582916

commit v4 on v3

--- a/solution.py
+++ b/solution.py
@@ -194,9 +194,10 @@
     )
 
 
-def solver_state(group):
+def solver_state(group, table=True):
     wide = PLANES * SIDE
-    return quad_state() * (group // PLANES) + [pltpu.VMEM((2, wide, wide), jnp.bfloat16)]
+    states = quad_state() * (group // PLANES)
+    return states + [pltpu.VMEM((2, wide, wide), jnp.bfloat16)] if table else states
 
 
 def quad_parts(state):
@@ -389,12 +390,14 @@
 def solver_parts(state, group):
     table = state[-1]
     count = group // PLANES
-    size = (len(state) - 1) // count
+    size = len(quad_state())
     quads = [quad_parts(state[size * q:size * q + size]) for q in range(count)]
 
     def clear():
         for quad in quads:
             quad[0]()
+
+    def tables():
         for way in range(2):
             table[way] = interleave(table.shape[1:], way == 1)
 
@@ -424,11 +427,12 @@
         for q, (_, _, total_of, _, settle, _, coefficients, *_) in enumerate(quads):
             settle(ITERS - 1, total_of(carry[q][0]) if q else carry[q][0], *carry[q][1:])
             coefficients()
-        for q, (*_, voltages, finish) in enumerate(quads):
+        for *_, voltages, _ in quads:
             voltages()
+        for q, (*_, finish) in enumerate(quads):
             finish(lambda w, cut, tile, q=q: store(PLANES * q + w, cut, tile), table.at[1])
 
-    return clear, solve
+    return clear, tables, solve
 
 
 def spans_of(rows, cols):
@@ -522,7 +526,7 @@
     raw, halos = refs[:3], dict(zip(SHIFTS, refs[3:11]))
     out, outs = refs[11], dict(zip(SHIFTS, refs[12:20]))
     bufs, sems, ext, acc, out_sem, staged, solved = refs[20:23], *refs[23:29]
-    clear, solve = solver_parts(refs[29:], PLANES)
+    clear, tables, solve = solver_parts(refs[29:], PLANES)
 
     def copies(slot, at):
         top, left = corner_of(centers, slot, rows, cols)
@@ -539,6 +543,7 @@
     count = live[0]
     acc[...] = jnp.zeros_like(acc)
     clear()
+    tables()
     spans = spans_of(rows, cols)
     for which in range(2):
         for dr in (-1, 1):
@@ -885,10 +890,10 @@
 
 def trade_kernel(windows, flag, *refs):
     pieces = dict(zip(SHIFTS, refs[:8]))
-    cur, outs, flag_out = refs[8], dict(zip(SHIFTS, refs[9:17])), refs[17]
-    halos = dict(zip(SHIFTS, refs[18:26]))
-    flag_landed, send_sems, recv_sems, flag_send, flag_recv = refs[26:31]
-    clear, solve = solver_parts(refs[31:], GROUP)
+    cur, outs, flag_out, table = refs[8], dict(zip(SHIFTS, refs[9:17])), *refs[17:19]
+    halos = dict(zip(SHIFTS, refs[19:27]))
+    flag_landed, send_sems, recv_sems, flag_send, flag_recv = refs[27:32]
+    clear, tables, solve = solver_parts([*refs[32:], table], GROUP)
     found = neighbours()
     peers = peers_along("row")
     for at in SHIFTS:
@@ -901,6 +906,7 @@
     for copy in shared:
         copy.start()
     clear()
+    tables()
 
     def store(b, cut, current):
         cur[b, cut, :] = current
@@ -918,13 +924,15 @@
     return jnp.concatenate((to_high if dc < 0 else to_low)(packed), axis=0)
 
 
-def rest_kernel(rows, cols, centers, live, order, windows, inner_cur, *refs):
-    halos, out, outs = dict(zip(SHIFTS, refs[:8])), refs[8], dict(zip(SHIFTS, refs[9:17]))
-    acc, out_sem, staged, solved = refs[17:21]
-    clear, solve = solver_parts(refs[21:], GROUP)
+def rest_kernel(rows, cols, centers, live, order, windows, inner_cur, table, *refs):
+    halos, acc, outs = dict(zip(SHIFTS, refs[:8])), refs[8], dict(zip(SHIFTS, refs[9:17]))
+    staged, solved = refs[17:19]
+    clear, _, solve = solver_parts([*refs[19:], table], GROUP)
+    solve_few = solver_parts([*refs[19:], table], PLANES)[2]
     slots = centers.shape[1]
     inner = order[1, 0]
     ready_count = jnp.minimum(inner, GROUP)
+    kept = jnp.minimum(inner, GROUP + PLANES)
     acc[...] = jnp.zeros_like(acc)
     clear()
     row_id = lax.broadcasted_iota(jnp.int32, (SIDE, SIDE), 0)
@@ -1002,9 +1010,9 @@
                     tile = pltpu.roll(tile, lax.rem(2 * SIDE - down[at[0]], SIDE), 0)
                     outs[at][order[2 + d, slot]] = tile[RAD:] if at[0] < 0 else tile[:RAD]
 
-    def solve_group(group, _):
-        first = ready_count + group * GROUP
-        size = jnp.minimum(live[0] - first, GROUP)
+    def solve_some(first, few):
+        bound, solver = (PLANES, solve_few) if few else (GROUP, solve)
+        size = jnp.minimum(live[0] - first, bound)
 
         def ready(b, _):
             n = seat(first + jnp.minimum(b, size - 1))
@@ -1023,25 +1031,34 @@
             give(b, slot)
             return 0
 
-        lax.fori_loop(0, GROUP, ready, 0)
-        solve(lambda b, cut: (staged[0, b, cut, :], staged[1, b, cut, :]), store)
+        lax.fori_loop(0, bound, ready, 0)
+        solver(lambda b, cut: (staged[0, b, cut, :], staged[1, b, cut, :]), store)
         lax.fori_loop(0, size, done, 0)
+
+    left_over = live[0] - kept
+    many = (left_over + GROUP - PLANES - 1) // GROUP
+
+    def solve_group(group, _):
+        solve_some(kept + group * GROUP, False)
         return 0
 
-    lax.fori_loop(0, (live[0] - ready_count + GROUP - 1) // GROUP, solve_group, 0)
-    copy = pltpu.make_async_copy(acc.at[pl.ds(RAD, rows), pl.ds(LANES, cols)], out, out_sem)
-    copy.start()
+    lax.fori_loop(0, many, solve_group, 0)
+
+    @pl.when(left_over > many * GROUP)
+    def _():
+        solve_some(kept + many * GROUP, True)
+
     spans = spans_of(rows, cols)
     for dr, dc in SHIFTS[4:]:
         tile = acc[spans[dr][0], spans[dc][1]]
         outs[(dr, dc)][...] = pack_high(tile) if dc < 0 else pack_low(tile)
-    copy.wait()
-
-
-def reply_kernel(flag, *refs):
-    pieces, outs, flag_out = dict(zip(SHIFTS, refs[:8])), dict(zip(SHIFTS, refs[8:16])), refs[16]
-    halos = dict(zip(SHIFTS, refs[17:25]))
-    flag_landed, send_sems, recv_sems, flag_send, flag_recv = refs[25:]
+
+
+def reply_kernel(windows, table, flag, *refs):
+    pieces, outs, flag_out, cur = dict(zip(SHIFTS, refs[:8])), dict(zip(SHIFTS, refs[8:16])), *refs[16:18]
+    halos = dict(zip(SHIFTS, refs[18:26]))
+    flag_landed, send_sems, recv_sems, flag_send, flag_recv = refs[26:31]
+    clear, _, solve = solver_parts([*refs[31:], table], PLANES)
     found = neighbours()
     peers = peers_along("col")
     for at in SHIFTS:
@@ -1053,6 +1070,12 @@
     shared = share_flag(flag, flag_landed, peers, flag_send, flag_recv)
     for copy in shared:
         copy.start()
+    clear()
+
+    def store(b, cut, current):
+        cur[b, cut, :] = current
+
+    solve(lambda b, cut: (windows[0, GROUP + b, cut, :], windows[1, GROUP + b, cut, :]), store)
     for copy in shared:
         copy.wait()
     flag_out[...] = largest(flag, flag_landed, peers)
@@ -1061,12 +1084,10 @@
         outs[at][...] = halos[at][...]
 
 
-def settle_kernel(rows, cols, meta, order, *refs):
-    halos = dict(zip(SHIFTS, refs[1:9]))
-    out, acc, out_sem = refs[9], refs[10], refs[11]
-    fetch = pltpu.make_async_copy(out, acc.at[pl.ds(RAD, rows), pl.ds(LANES, cols)], out_sem)
-    fetch.start()
-    fetch.wait()
+def settle_kernel(rows, cols, centers, meta, order, *refs):
+    cur, halos = refs[0], dict(zip(SHIFTS, refs[1:9]))
+    out, acc, out_sem = refs[10:]
+    own = acc.at[pl.ds(RAD, rows), pl.ds(LANES, cols)]
     blank = jnp.zeros((RAD, SIDE), jnp.float32)
     for d, at in enumerate(MAIN):
         def add(k, _, d=d, at=at):
@@ -1085,6 +1106,13 @@
             return 0
 
         lax.fori_loop(0, order[1, 1 + d], add, 0)
+    def place(b, _):
+        slot = order[0, GROUP + b]
+        top, left = lax.rem(centers[0, slot], rows) - RAD, lax.rem(centers[1, slot], cols) - RAD
+        add_window(acc, cur[b], top, left)
+        return 0
+
+    lax.fori_loop(0, jnp.clip(order[1, 0] - GROUP, 0, PLANES), place, 0)
     for dr, dc in SHIFTS[4:]:
         first, second = (to_low if dc < 0 else to_high)(halos[(dr, dc)][...])
         low = lanes_of(first.shape) < RAD
@@ -1094,7 +1122,7 @@
         for n, part in enumerate((first, second)):
             span = slice(r + RAD // 2 * n, r + RAD // 2 * n + RAD // 2), slice(c, c + LANES)
             acc[span] = acc[span] + jnp.where(keep, part, 0.0)
-    store = pltpu.make_async_copy(acc.at[pl.ds(RAD, rows), pl.ds(LANES, cols)], out, out_sem)
+    store = pltpu.make_async_copy(own, out, out_sem)
     store.start()
     store.wait()
 
@@ -1211,54 +1239,57 @@
         trade_kernel,
         out_shape=[jax.ShapeDtypeStruct((GROUP, SIDE, SIDE), f32)]
         + [jax.ShapeDtypeStruct(shape, f32) for shape in twice]
-        + [flag_shape],
+        + [flag_shape, jax.ShapeDtypeStruct((2, PLANES * SIDE, PLANES * SIDE), jnp.bfloat16)],
         in_specs=[vmem] * 10,
-        out_specs=[vmem] * 10,
+        out_specs=[vmem] * 11,
         scratch_shapes=[pltpu.VMEM(shape, f32) for shape in twice]
         + [pltpu.VMEM((row_peers, 8, LANES), i32), dma((8,)), dma((8,)), dma((row_peers,)), dma((row_peers,))]
-        + solver_state(GROUP),
+        + solver_state(GROUP, False),
         compiler_params=pltpu.CompilerParams(vmem_limit_bytes=32 << 20, collective_id=1, has_side_effects=True),
         name="trade",
     )(windows, flag, *pieces)
-    halos, flag = rest[:8], rest[8]
-
-    merged, *pieces = pl.pallas_call(
+    halos, flag, table = rest[:8], rest[8], rest[9]
+
+    acc_shape = jax.ShapeDtypeStruct((rows + SIDE, cols + WIDE), f32)
+    acc, *pieces = pl.pallas_call(
         functools.partial(rest_kernel, rows, cols),
-        out_shape=[jax.ShapeDtypeStruct((rows, cols), f32)]
-        + [jax.ShapeDtypeStruct(piece[at], f32) for at in SHIFTS],
-        in_specs=[smem, smem, smem] + [vmem] * 10,
-        out_specs=[hbm] + [vmem] * 8,
-        scratch_shapes=[pltpu.VMEM((rows + SIDE, cols + WIDE), f32), dma]
-        + [pltpu.VMEM((2, GROUP, SIDE, SIDE), f32), pltpu.VMEM((GROUP, SIDE, SIDE), f32)]
-        + solver_state(GROUP),
+        out_shape=[acc_shape] + [jax.ShapeDtypeStruct(piece[at], f32) for at in SHIFTS],
+        in_specs=[smem, smem, smem] + [vmem] * 11,
+        out_specs=[vmem] * 9,
+        scratch_shapes=[pltpu.VMEM((2, GROUP, SIDE, SIDE), f32), pltpu.VMEM((GROUP, SIDE, SIDE), f32)]
+        + solver_state(GROUP, False),
         compiler_params=pltpu.CompilerParams(vmem_limit_bytes=40 << 20),
         name="rest",
-    )(centers, live, order, windows, inner_cur, *halos)
-
-    *halos, flag = pl.pallas_call(
+    )(centers, live, order, windows, inner_cur, table, *halos)
+
+    *halos, flag, late_cur = pl.pallas_call(
         reply_kernel,
-        out_shape=[jax.ShapeDtypeStruct(piece[at], f32) for at in SHIFTS] + [flag_shape],
-        in_specs=[vmem] * 9,
-        out_specs=[vmem] * 9,
+        out_shape=[jax.ShapeDtypeStruct(piece[at], f32) for at in SHIFTS]
+        + [flag_shape, jax.ShapeDtypeStruct((PLANES, SIDE, SIDE), f32)],
+        in_specs=[vmem] * 11,
+        out_specs=[vmem] * 10,
         scratch_shapes=[pltpu.VMEM(piece[at], f32) for at in SHIFTS]
-        + [pltpu.VMEM((col_peers, 8, LANES), i32), dma((8,)), dma((8,)), dma((col_peers,)), dma((col_peers,))],
-        compiler_params=pltpu.CompilerParams(vmem_limit_bytes=8 << 20, collective_id=2, has_side_effects=True),
+        + [pltpu.VMEM((col_peers, 8, LANES), i32), dma((8,)), dma((8,)), dma((col_peers,)), dma((col_peers,))]
+        + solver_state(PLANES, False),
+        compiler_params=pltpu.CompilerParams(vmem_limit_bytes=20 << 20, collective_id=2, has_side_effects=True),
         name="reply",
-    )(flag, *pieces)
-
-    def quick():
-        return pl.pallas_call(
-            functools.partial(settle_kernel, rows, cols),
-            out_shape=jax.ShapeDtypeStruct((rows, cols), f32),
-            in_specs=[smem, smem, hbm] + [vmem] * 8,
-            out_specs=hbm,
-            scratch_shapes=[pltpu.VMEM((rows + SIDE, cols + WIDE), f32), dma],
-            input_output_aliases={2: 0},
-            compiler_params=pltpu.CompilerParams(vmem_limit_bytes=16 << 20),
-            name="settle",
-        )(meta, order, merged, *halos)
-
-    return lax.cond(flag[0, 0] > 0, lambda: slow_path(rows, cols, centers, live, raster), quick)
+    )(windows, table, flag, *pieces)
+
+    out, _ = pl.pallas_call(
+        functools.partial(settle_kernel, rows, cols),
+        out_shape=[jax.ShapeDtypeStruct((rows, cols), f32), acc_shape],
+        in_specs=[smem, smem, smem] + [vmem] * 10,
+        out_specs=[hbm, vmem],
+        scratch_shapes=[dma],
+        input_output_aliases={12: 1},
+        compiler_params=pltpu.CompilerParams(vmem_limit_bytes=16 << 20),
+        name="settle",
+    )(centers, meta, order, late_cur, *halos, acc)
+
+    def again(carry):
+        return jnp.int32(0), slow_path(rows, cols, centers, live, raster)
+
+    return lax.while_loop(lambda carry: carry[0] > 0, again, (flag[0, 0], out))[1]
 
 
 def solution(mesh):

time: 66.8 us -> 61.1 us (0.915)
  the two profiles are of different devices: /device:TPU:0 before, /device:TPU:3 now
where the time goes in v4:
time: 61.1 us; the launch traced here: 61.7 us
  Pallas kernels  59.6 us (98%)
  between operations  0.88 us (1%)
  loops' own time  0.64 us (1%)
    pallas_call x1, Pallas kernels, local(): pl.pallas_call(reply_kernel, out_shape=[jax.ShapeDtypeStruct(piece[at], f...  29 us
    pallas_call x1, Pallas kernels, local(): pl.pallas_call(trade_kernel, out_shape=[jax.ShapeDtypeStruct((GROUP, SIDE...  17.1 us
    pallas_call x1, Pallas kernels, local(): pl.pallas_call(functools.partial(pack_kernel, rows, cols), out_shape=[jax...  4.51 us
    pallas_call x1, Pallas kernels, local(): pl.pallas_call(meta_kernel, out_shape=jax.ShapeDtypeStruct((len(MAIN), 8,...  4.34 us
    pallas_call x1, Pallas kernels, local(): pl.pallas_call(functools.partial(settle_kernel, rows, cols), out_shape=[j...  3.29 us
    pallas_call x1, Pallas kernels, local(): pl.pallas_call(functools.partial(rest_kernel, rows, cols), out_shape=[acc...  1.35 us

profile of v4, /device:TPU:3, one launch (start us, length us, event | category | flops | bytes accessed | tf_op | source)
XLA Modules:
  0.0 61.7 jit_solution(3007218921522958123)
XLA Ops:
  0.7 4.3 %meta.1 = s32[4,8,128]{2,1,0:T(8,128)S(1)} custom-call(s32[2,16]{1,0:T(2,128)} %bitcast.2, s32[1]{0:T(128)S(6)} %copy.17.live), custom_call_target="tpu_custom_call" | custom-call | tf_op jit(solution)/shard_map/meta/pallas_call | solution.py:1212
  5.0 0.0 copy-start.4
  5.0 4.5 %pack.1 = (f32[2,16,128,128]{3,2,1,0:T(8,128)S(1)}, s32[10,16]{1,0:T(8,128)S(1)}, f32[2,4,64,128]{3,2,1,0:T(8,128)S(1)}, f32[2,4,64,128]{3,2,1,0:T(8,128)S(1)}, ...) custom-call(s32[2,16]{1,0:T(2,128)} %bitcast.3, ...), custom_call_target="tpu_custom_call" | custom-call | tf_op jit(solution)/shard_map/pack/pallas_call | solution.py:1222
  9.5 17.1 %trade.1 = (f32[8,128,128]{2,1,0:T(8,128)S(1)}, f32[2,4,64,128]{3,2,1,0:T(8,128)S(1)}, f32[2,4,64,128]{3,2,1,0:T(8,128)S(1)}, f32[2,4,64,128]{3,2,1,0:T(8,128)S(...) custom-call(f32[2,16,128,128]{3,2,1,0:T(8,128)S(1)} %get-tuple-eleme, ...), custom_call_target="tpu_custom_call" | custom-call | tf_op jit(solution)/shard_map/trade/pallas_call | solution.py:1238
  26.7 0.0 copy-done.4
  26.7 1.4 %rest.1 = (f32[1152,1280]{1,0:T(8,128)S(1)}, f32[4,64,128]{2,1,0:T(8,128)S(1)}, f32[4,64,128]{2,1,0:T(8,128)S(1)}, f32[4,64,128]{2,1,0:T(8,128)S(1)}, f32[4,64,1...) custom-call(s32[2,16]{1,0:T(2,128)S(1)} %bitcast.4, ...), custom_call_target="tpu_custom_call" | custom-call | tf_op jit(solution)/shard_map/rest/pallas_call | solution.py:1254
  28.0 29.0 %reply.1 = (f32[4,64,128]{2,1,0:T(8,128)S(1)}, f32[4,64,128]{2,1,0:T(8,128)S(1)}, f32[4,64,128]{2,1,0:T(8,128)S(1)}, f32[4,64,128]{2,1,0:T(8,128)S(1)}, f32[32,1...) custom-call(f32[2,16,128,128]{3,2,1,0:T(8,128)S(1)} %get-tuple-eleme, ...), custom_call_target="tpu_custom_call" | custom-call | tf_op jit(solution)/shard_map/reply/pallas_call | solution.py:1265
  57.1 0.5 slice.3
  57.6 3.3 %settle.1 = (f32[1024,1024]{1,0:T(8,128)}, f32[1152,1280]{1,0:T(8,128)S(1)}) custom-call(s32[2,16]{1,0:T(2,128)S(1)} %bitcast.5, s32[4,8,128]{2,1,0:T(8,128)S(1)} %meta.1, s32[10,16]{1,0:T(8,128)S(1)} %get-tuple-element.119.order, f32[4,128,128]{2,1,0:T(8,128)S(1)} %get-tuple-element.138.refs_0_, ...), custom_call_target="tpu_custom_call", output_to_operand_aliasing={{1}: (12, {})} | custom-call | tf_op jit(solution)/shard_map/settle/pallas_call | solution.py:1278
  60.9 0.6 %while.9 = (s32[]{:T(128)}, f32[1024,1024]{1,0:T(8,128)}, f32[1024,1024]{1,0:T(8,128)}, s32[1024,1024]{1,0:T(8,128)}, s32[1024,1024]{1,0:T(8,128)}, /*index=5*/s32[2,16]{1,0:T(2,128)S(1)}, s32[1]{0:T(128)}) while((s32[]{:T(128)}, f32[1024,1024]{1,0:T(8,128)}, f32[1024,1024]{1,0:T(8,128)}, s32[1024,1024]{1,0:T(8,128)}, s32[1024,1024]{1,0:T(8,128)}, ...), condition=%region_1.0_spmd, body=%region_0.0_spmd | while | flops 1 | bytes 67109048 | solution.py:1292
Async XLA Ops:
  5.0 21.7 %copy-start.4 = (s32[16,2]{0,1:T(2,128)S(1)}, s32[16,2]{0,1:T(2,128)}, u32[]{:S(2)}) copy-start(s32[16,2]{0,1:T(2,128)} %param.10) | copy-start | bytes 388
